TPU v7x, 128 devices: a whole 4x4x4 slice. The times are simulated.
128 devices in a mesh: seq: 64 (over z, y, x), head: 2 (over core).
Axes of the slice: x: 4, y: 4, z: 4, core: 2. Of those that a mesh axis runs over, the one named last changes fastest.
Arguments:
- acceptance_signal: bfloat16 [32768, 2048], P(('seq', 'head')), may hold values from -6 to 6
- lookup_entries: bfloat16 [32768, 2048], P(('seq', 'head')), may hold values from -6 to 6
- content_entries: bfloat16 [32768, 2048], P(('seq', 'head')), may hold values from -6 to 6
- fading_exponent_table: bfloat16 [32768, 2048], P(('seq', 'head')), may hold values from -17 to 0
- raw_control_signal: bfloat16 [32768, 2048], P(('seq', 'head')), may hold values from -6 to 6
- current_token_reward: float32 [32, 64], P('head'), may hold values from -1 to 1
- slice_scaling_factor: float32 [2048], P('head'), may hold values from 0.1 to 1.9
- result_mapping: bfloat16 [2048, 4096], P('head'), may hold values from -0.125 to 0.125
Outputs:
- time_mixed: bfloat16 [32768, 4096], P(('seq', 'head'))
All inputs are finite; a program needn't handle non-finite values.
Results may differ from a plain program's by a relative error of at most 0.009.
Values may be sent and summed in bfloat16 or wider, within the bound.
No kernel may reach another device: no remote copies, remote signals or barrier semaphores. Data moves between devices by JAX's collectives and lax.ppermute only.
A program may use at most 192 MiB of HBM per device.

v0:
```python
import functools

import jax
import jax.numpy as jnp
from jax import lax
from jax.experimental import pallas as pl
from jax.experimental.pallas import tpu as pltpu
from jax.sharding import Mesh
from jax.sharding import PartitionSpec as P

BLOCK = 128
HALF = 64
PAIR = 128
WIDE = 256
SEQ_HEAD = ("seq_0", "seq_1", "seq_2", "head")
EPS = 1e-05
BF = jnp.bfloat16
F32 = jnp.float32


def mm(a, b):
    return lax.dot_general(a, b, (((1,), (0,)), ((), ())), preferred_element_type=F32)


def mm_nt(a, b):
    return lax.dot_general(a, b, (((1,), (1,)), ((), ())), preferred_element_type=F32)


def mm_tn(a, b):
    return lax.dot_general(a, b, (((0,), (0,)), ((), ())), preferred_element_type=F32)


def grid2(rows, cols):
    return (
        lax.broadcasted_iota(jnp.int32, (rows, cols), 0),
        lax.broadcasted_iota(jnp.int32, (rows, cols), 1),
    )


def two_parts(x):
    hi = x.astype(BF)
    return hi, (x - hi.astype(F32)).astype(BF)


def head_ones(scale):
    row, col = grid2(WIDE, WIDE)
    return jnp.where(row // HALF == col // HALF, scale, 0.0).astype(BF)


def state_kernel(k_ref, v_ref, w_ref, msg_ref):
    tokens = k_ref.shape[0]
    log_decay = -jnp.exp(w_ref[...].astype(F32))
    hi, lo = two_parts(log_decay)
    row, col = grid2(tokens, tokens)
    later = jnp.where(col > row, 1.0, 0.0).astype(BF)
    after = mm(later, hi) + mm(later, lo)
    key_end = (k_ref[...].astype(F32) * jnp.exp(after)).astype(BF)
    total = after[0:1] + log_decay[0:1]
    state = mm_tn(v_ref[...], key_end)
    tot_hi, tot_lo = two_parts(total)
    tot_hi, tot_lo = tot_hi.astype(F32), tot_lo.astype(F32)
    first = lax.broadcasted_iota(jnp.int32, (HALF, PAIR), 1) < HALF
    sub = lax.broadcasted_iota(jnp.int32, (8, PAIR), 0)
    for p in range(WIDE // PAIR):
        at = p * PAIR
        both = jnp.where(
            first, state[at : at + HALF, at : at + PAIR], state[at + HALF : at + PAIR, at : at + PAIR]
        )
        logs = jnp.where(
            sub == 0,
            jnp.broadcast_to(tot_hi[:, at : at + PAIR], (8, PAIR)),
            jnp.where(sub == 1, jnp.broadcast_to(tot_lo[:, at : at + PAIR], (8, PAIR)), 0.0),
        )
        rows = jnp.concatenate(
            [both.reshape(8, 8, PAIR), jnp.broadcast_to(logs[None], (8, 8, PAIR))], axis=1
        )
        msg_ref[p * 8 : p * 8 + 8] = rows.astype(BF)


def local_kernel(r_ref, k_ref, v_ref, w_ref, u_ref, out_ref, rin_ref):
    tokens = r_ref.shape[0]
    log_decay = -jnp.exp(w_ref[...].astype(F32))
    hi, lo = two_parts(log_decay)
    row, col = grid2(tokens, tokens)
    upto = jnp.where(col <= row, 1.0, 0.0).astype(BF)
    cum = mm(upto, hi) + mm(upto, lo)
    before = cum - log_decay
    r = r_ref[...].astype(F32)
    k = k_ref[...].astype(F32)
    v = v_ref[...]
    mid0, end0, mid1 = cum[63:64], cum[127:128], cum[191:192]
    r0 = r[:BLOCK] * jnp.exp(before[:BLOCK] - mid0)
    k0 = k[:BLOCK] * jnp.exp(mid0 - cum[:BLOCK])
    r1 = r[BLOCK:] * jnp.exp(before[BLOCK:] - mid1)
    k1 = k[BLOCK:] * jnp.exp(mid1 - cum[BLOCK:])
    r1c = r1 * jnp.exp(mid1 - end0)
    k0c = k0 * jnp.exp(end0 - mid0)
    rin_ref[:BLOCK] = (r0 * jnp.exp(mid0)).astype(BF)
    rin_ref[BLOCK:] = (r1c * jnp.exp(end0)).astype(BF)
    own = mm((r * u_ref[...] * k).astype(BF), head_ones(1.0)) * v.astype(F32)
    r0, k0, r1, k1, r1c, k0c = (x.astype(BF) for x in (r0, k0, r1, k1, r1c, k0c))
    lane = lax.broadcasted_iota(jnp.int32, (BLOCK, PAIR), 1)
    first = lane < HALF
    zero = jnp.zeros((BLOCK, PAIR), BF)
    row, col = grid2(BLOCK, BLOCK)
    strict = row > col

    def stacked(x):
        return jnp.concatenate([jnp.where(first, x, zero), jnp.where(first, zero, x)], axis=0)

    def side(scores, masked):
        a, b = scores[:BLOCK], scores[BLOCK:]
        if masked:
            a, b = jnp.where(strict, a, 0.0), jnp.where(strict, b, 0.0)
        return jnp.concatenate([a, b], axis=1).astype(BF)

    for p in range(WIDE // PAIR):
        s = slice(p * PAIR, (p + 1) * PAIR)
        s00 = side(mm_nt(stacked(r0[:, s]), k0[:, s]), True)
        s10 = side(mm_nt(stacked(r1c[:, s]), k0c[:, s]), False)
        s11 = side(mm_nt(stacked(r1[:, s]), k1[:, s]), True)
        v0, v1 = stacked(v[:BLOCK, s]), stacked(v[BLOCK:, s])
        out_ref[:BLOCK, s] = mm(s00, v0) + own[:BLOCK, s]
        out_ref[BLOCK:, s] = mm(s10, v0) + mm(s11, v1) + own[BLOCK:, s]


def scan_kernel(msg_ref, out_ref):
    groups = msg_ref.shape[0]
    state = jnp.zeros((8, PAIR), F32)
    for g in range(groups):
        block = msg_ref[g].astype(F32)
        out_ref[g] = state.astype(BF)
        decay = jnp.exp(block[8:9] + block[9:10])
        state = state * decay + block[:8]


def finish_kernel(c_ref, out_ref, rin_ref, s_ref, g_ref, gain_ref, w1_ref, w2_ref, y_ref, gated):
    step = pl.program_id(0)
    chunks = gated.shape[0]

    @pl.when(step < chunks)
    def _():
        lane = lax.broadcasted_iota(jnp.int32, (HALF, PAIR), 1)
        first = lane < HALF
        zero = jnp.zeros((HALF, PAIR), BF)
        a, b = s_ref[0], s_ref[1]
        entering = jnp.concatenate(
            [
                jnp.concatenate([jnp.where(first, a, zero), zero], axis=1),
                jnp.concatenate([jnp.where(first, zero, a), zero], axis=1),
                jnp.concatenate([zero, jnp.where(first, b, zero)], axis=1),
                jnp.concatenate([zero, jnp.where(first, zero, b)], axis=1),
            ],
            axis=0,
        )
        wkv = out_ref[...] + mm_nt(rin_ref[...], entering)
        share = head_ones(1.0 / HALF)
        hi, lo = two_parts(wkv)
        centred = wkv - (mm(hi, share) + mm(lo, share))
        var = mm((centred * centred).astype(BF), share)
        gate = g_ref[...].astype(F32)
        silu = 0.5 * gate * (1.0 + jnp.tanh(0.5 * gate))
        gated[step] = (centred * lax.rsqrt(var + EPS) * gain_ref[...] * silu).astype(BF)

    @pl.when(step >= chunks)
    def _():
        half = chunks // 2
        acc = jnp.zeros(y_ref.shape, F32)
        for j in range(half):
            acc += mm(gated[j], w1_ref[j * WIDE : (j + 1) * WIDE])
        for j in range(half):
            acc += mm(gated[half + j], w2_ref[j * WIDE : (j + 1) * WIDE])
        y_ref[...] = acc.astype(BF)


def params(*semantics):
    return pltpu.CompilerParams(dimension_semantics=semantics, vmem_limit_bytes=48 << 20)


def shards(r, k, v, w, g, bonus, gain, weight):
    tokens, width = r.shape
    chunks = width // WIDE
    groups = lax.axis_size(SEQ_HEAD)
    pairs = width // PAIR
    core = lax.axis_index("head")
    swap = [(0, 1), (1, 0)]
    other_weight = lax.ppermute(weight, "head", swap)
    small = jnp.stack([bonus.reshape(-1), gain])
    other_small = lax.ppermute(small, "head", swap)
    low = jnp.where(core == 0, small, other_small)
    high = jnp.where(core == 0, other_small, small)
    small = jnp.concatenate([low, high], axis=1)
    bonus, gain = small[0:1], small[1:2]

    block = pl.BlockSpec((tokens, WIDE), lambda i: (0, i))
    per = groups // chunks
    msg = pl.pallas_call(
        state_kernel,
        grid=(chunks,),
        in_specs=[block] * 3,
        out_specs=pl.BlockSpec((per, 16, PAIR), lambda i: (i, 0, 0)),
        out_shape=jax.ShapeDtypeStruct((groups, 16, PAIR), BF),
        compiler_params=params("arbitrary"),
        cost_estimate=pl.CostEstimate(flops=4 << 30, bytes_accessed=4 << 20, transcendentals=1 << 20),
        name="state",
    )(k, v, w)
    msg = lax.all_to_all(msg, SEQ_HEAD, split_axis=0, concat_axis=0, tiled=True)

    def local(first, count):
        blk = pl.BlockSpec((tokens, WIDE), lambda i: (0, i + first))
        out_blk = pl.BlockSpec((tokens, WIDE), lambda i: (0, i))
        return pl.pallas_call(
            local_kernel,
            grid=(count,),
            in_specs=[blk] * 4 + [pl.BlockSpec((1, WIDE), lambda i: (0, i + first))],
            out_specs=[out_blk, out_blk],
            out_shape=[
                jax.ShapeDtypeStruct((tokens, count * WIDE), F32),
                jax.ShapeDtypeStruct((tokens, count * WIDE), BF),
            ],
            compiler_params=params("arbitrary"),
            cost_estimate=pl.CostEstimate(
                flops=8 << 30, bytes_accessed=10 << 20, transcendentals=4 << 20
            ),
            name="local",
        )(r, k, v, w, bonus)

    out, rin = local(0, chunks)
    entering = pl.pallas_call(
        scan_kernel,
        out_shape=jax.ShapeDtypeStruct((groups, 8, PAIR), BF),
        compiler_params=params(),
        name="scan",
    )(msg)
    entering = lax.all_to_all(entering, SEQ_HEAD, split_axis=0, concat_axis=0, tiled=True)
    entering = entering.reshape(pairs, HALF, PAIR)

    cols = weight.shape[1]
    tile = 512
    tiles = cols // tile

    def chan(i, c):
        return lax.rem(jnp.minimum(i, chunks - 1) + c[0] * (chunks // 2), chunks)

    chan_block = pl.BlockSpec((tokens, WIDE), lambda i, c: (0, chan(i, c)))
    w_block = pl.BlockSpec((width // 2, tile), lambda i, c: (0, jnp.maximum(i - chunks, 0)))
    return pl.pallas_call(
        finish_kernel,
        grid_spec=pltpu.PrefetchScalarGridSpec(
            num_scalar_prefetch=1,
            grid=(chunks + tiles,),
            in_specs=[
                chan_block,
                chan_block,
                pl.BlockSpec((2, HALF, PAIR), lambda i, c: (chan(i, c), 0, 0)),
                chan_block,
                pl.BlockSpec((1, WIDE), lambda i, c: (0, chan(i, c))),
                w_block,
                w_block,
            ],
            out_specs=pl.BlockSpec((tokens, tile), lambda i, c: (0, jnp.maximum(i - chunks, 0))),
            scratch_shapes=[pltpu.VMEM((chunks, tokens, WIDE), BF)],
        ),
        out_shape=jax.ShapeDtypeStruct((tokens, cols), BF),
        compiler_params=params("arbitrary"),
        name="finish",
    )(core.reshape(1).astype(jnp.int32), out, rin, entering, g, gain, weight, other_weight)


def solution(mesh):
    torus = Mesh(mesh.devices.reshape(4, 4, 4, mesh.shape["head"]), SEQ_HEAD)
    in_specs = (P(SEQ_HEAD, None),) * 5 + (P("head", None), P("head"), P("head", None))
    return jax.shard_map(
        shards, mesh=torus, in_specs=in_specs, out_specs=P(SEQ_HEAD, None), check_vma=False
    )
```

profile of v0, /device:TPU:1, one launch (start us, length us, event | category | flops | bytes accessed | tf_op | source)
XLA Modules:
  0.0 71.1 jit_solution(8904913042424298189)
XLA Ops:
  0.0 0.0 copy-start.2
  0.0 1.4 %collective-permute-start.1 = (bf16[1024,4096]{1,0:T(8,128)(2,1)}, bf16[1024,4096]{1,0:T(8,128)(2,1)}, u32[]{:S(2)}, u32[]{:S(2)}) collective-permute-start(bf16[1024,4096]{1,0:T(8,128)(2,1)} %w1_ref.1), channel_id=1, source_target_pairs={{0,1},{1,0},{2,3},{3,2},{4,5},{5,4},{6,7},{7,6},{8,9},{9,8},{10,11... | collective-permute-start | bytes 25165832 | tf_op jit(solution)/shard_map/ppermute | solution.py:187
  1.4 0.0 copy-start.3
  1.4 1.2 %copy-done.3 = bf16[256,2048]{1,0:T(8,128)(2,1)S(1)} copy-done((bf16[256,2048]{1,0:T(8,128)(2,1)S(1)}, bf16[256,2048]{1,0:T(8,128)(2,1)}, u32[]{:S(2)}) %copy-start.3) | copy-done | bytes 1048600
  2.6 1.2 %copy-done.5 = bf16[256,2048]{1,0:T(8,128)(2,1)S(1)} copy-done((bf16[256,2048]{1,0:T(8,128)(2,1)S(1)}, bf16[256,2048]{1,0:T(8,128)(2,1)}, u32[]{:S(2)}) %copy-start.5) | copy-done | bytes 1048600
  3.8 0.0 copy-start.7
  3.8 1.2 %copy-done.7 = bf16[256,2048]{1,0:T(8,128)(2,1)S(1)} copy-done((bf16[256,2048]{1,0:T(8,128)(2,1)S(1)}, bf16[256,2048]{1,0:T(8,128)(2,1)}, u32[]{:S(2)}) %copy-start.7) | copy-done | bytes 1048600
  5.1 0.0 copy-start.10
  5.1 0.0 copy-start.9
  5.1 5.3 %state.1 = bf16[128,16,128]{2,1,0:T(8,128)(2,1)} custom-call(bf16[256,2048]{1,0:T(8,128)(2,1)S(1)} %copy-done.3, bf16[256,2048]{1,0:T(8,128)(2,1)S(1)} %copy-done.5, bf16[256,2048]{1,0:T(8,128)(2,1)S(1)} %copy-done.7), custom_call_target="tpu_custom_call" | custom-call | flops 4294967296 | bytes 4194304 | tf_op jit(solution)/shard_map/state/pallas_call | solution.py:197
  10.4 10.2 %all-to-all-start = ((bf16[128,16,128]{2,1,0:T(8,128)(2,1)}), bf16[128,16,128]{2,1,0:T(8,128)(2,1)S(1)}, u32[]{:S(2)}, u32[]{:S(2)}) async-start(bf16[128,16,128]{2,1,0:T(8,128)(2,1)} %state.1), calls=%async_computation | async-start | bytes 1048576 | tf_op jit(solution)/shard_map/all_to_all | solution.py:207
  20.6 0.0 copy-done.10
  20.6 0.1 stack_reshape.3
  20.7 0.0 copy-done.9
  20.7 1.1 %collective-permute-start = (f32[2,1024]{1,0:T(2,128)S(1)}, f32[2,1024]{1,0:T(2,128)S(1)}, u32[]{:S(2)}, u32[]{:S(2)}) collective-permute-start(f32[2,1024]{1,0:T(2,128)S(1)} %pad_maximum_fusion.1), channel_id=1, source_target_pairs={{0,1},{1,0},{2,3},{3,2},{4,5},{5,4},{6,7},{7,6},{8,9},{9,8},{10,11... | collective-permute-start | bytes 24584 | tf_op jit(solution)/shard_map/ppermute | solution.py:189
  21.8 0.8 %collective-permute-done = f32[2,1024]{1,0:T(2,128)S(1)} collective-permute-done((f32[2,1024]{1,0:T(2,128)S(1)}, f32[2,1024]{1,0:T(2,128)S(1)}, u32[]{:S(2)}, u32[]{:S(2)}) %collective-permute-start) | collective-permute-done | bytes 8224 | tf_op jit(solution)/shard_map/ppermute | solution.py:189
  22.7 11.5 %all-to-all-done.msg_ref = bf16[128,16,128]{2,1,0:T(8,128)(2,1)S(1)} async-done(((bf16[128,16,128]{2,1,0:T(8,128)(2,1)}), bf16[128,16,128]{2,1,0:T(8,128)(2,1)S(1)}, u32[]{:S(2)}, u32[]{:S(2)}) %all-to-all-start) | async-done | bytes 524320 | tf_op jit(solution)/shard_map/all_to_all | solution.py:207
  34.2 1.0 %scan.1 = bf16[128,8,128]{2,1,0:T(8,128)(2,1)} custom-call(bf16[128,16,128]{2,1,0:T(8,128)(2,1)S(1)} %all-to-all-done.msg_ref), custom_call_target="tpu_custom_call" | custom-call | tf_op jit(solution)/shard_map/scan/pallas_call | solution.py:229
  35.2 4.6 %all-to-all-start.1 = ((bf16[128,8,128]{2,1,0:T(8,128)(2,1)}), bf16[128,8,128]{2,1,0:T(8,128)(2,1)S(1)}, u32[]{:S(2)}, u32[]{:S(2)}) async-start(bf16[128,8,128]{2,1,0:T(8,128)(2,1)} %scan.1), calls=%async_computation.1 | async-start | bytes 524288 | tf_op jit(solution)/shard_map/all_to_all | solution.py:235
  39.8 0.0 copy-done.2
  39.8 0.0 copy-start.4
  39.8 1.2 %copy-done.4 = bf16[256,2048]{1,0:T(8,128)(2,1)S(1)} copy-done((bf16[256,2048]{1,0:T(8,128)(2,1)S(1)}, bf16[256,2048]{1,0:T(8,128)(2,1)}, u32[]{:S(2)}) %copy-start.4) | copy-done | bytes 1048600
  41.0 0.0 copy-start.6
  41.0 1.2 %copy-done.6 = bf16[256,2048]{1,0:T(8,128)(2,1)S(1)} copy-done((bf16[256,2048]{1,0:T(8,128)(2,1)S(1)}, bf16[256,2048]{1,0:T(8,128)(2,1)}, u32[]{:S(2)}) %copy-start.6) | copy-done | bytes 1048600
  42.3 1.2 %copy-done.8 = bf16[256,2048]{1,0:T(8,128)(2,1)S(1)} copy-done((bf16[256,2048]{1,0:T(8,128)(2,1)S(1)}, bf16[256,2048]{1,0:T(8,128)(2,1)}, u32[]{:S(2)}) %copy-start.8) | copy-done | bytes 1048600
  43.5 8.4 %local.1 = (f32[256,2048]{1,0:T(8,128)}, bf16[256,2048]{1,0:T(8,128)(2,1)S(1)}) custom-call(bf16[256,2048]{1,0:T(8,128)(2,1)S(1)} %copy-done.2, bf16[256,2048]{1,0:T(8,128)(2,1)S(1)} %copy-done.4, bf16[256,2048]{1,0:T(8,128)(2,1)S(1)} %copy-done.6, bf16[256,2048]{1,0:T(8,128)(2,1)S(1)} %copy-done.8, f32[1,2048]{1,0:T(1,128)S(1)} %get-tuple-element.10.u_ref), custom_call_target="tpu_custom_call" | custom-call | flops 8589934592 | bytes 10485760 | tf_op jit(solution)/shard_map/local/pallas_call | solution.py:212
  51.9 0.0 all-to-all-done.1
  51.9 0.0 collective-permute-done.1.w2_ref
  51.9 0.0 copy-done.1
  51.9 0.0 copy-start
  51.9 1.6 %copy-done = f32[256,2048]{1,0:T(8,128)S(1)} copy-done((f32[256,2048]{1,0:T(8,128)S(1)}, f32[256,2048]{1,0:T(8,128)}, u32[]{:S(2)}) %copy-start) | copy-done | bytes 2097176
  53.5 17.6 %finish.1 = bf16[256,4096]{1,0:T(8,128)(2,1)} custom-call(s32[1]{0:T(128)} %bitcast.c_ref, f32[256,2048]{1,0:T(8,128)S(1)} %copy-done, bf16[256,2048]{1,0:T(8,128)(2,1)S(1)} %get-tuple-element.8.rin_ref, bf16[16,64,128]{2,1,0:T(8,128)(2,1)S(1)} %bitcast.3, bf16[256,2048]{1,0:T(8,128)(2,1)S(1)} %copy-done.1, f32[1,2048]{1,0:T(1,128)S(1)} %get-tuple-element.9.gain_ref, ...), custom_call_target="tpu_custom_call" | custom-call | tf_op jit(solution)/shard_map/finish/pallas_call | solution.py:247
  (6 shorter events, 0.0 us)
Async XLA Ops:
  0.0 39.8 %copy-start.2 = (bf16[256,2048]{1,0:T(8,128)(2,1)S(1)}, bf16[256,2048]{1,0:T(8,128)(2,1)}, u32[]{:S(2)}) copy-start(bf16[256,2048]{1,0:T(8,128)(2,1)} %r_ref.1) | copy-start | bytes 3145732
  0.0 51.9 %collective-permute-start.1 = (bf16[1024,4096]{1,0:T(8,128)(2,1)}, bf16[1024,4096]{1,0:T(8,128)(2,1)}, u32[]{:S(2)}, u32[]{:S(2)}) collective-permute-start(bf16[1024,4096]{1,0:T(8,128)(2,1)} %w1_ref.1), channel_id=1, source_target_pairs={{0,1},{1,0},{2,3},{3,2},{4,5},{5,4},{6,7},{7,6},{8,9},{9,8},{10,11... | collective-permute-start | bytes 25165832 | tf_op jit(solution)/shard_map/ppermute | solution.py:187
  1.4 1.2 %copy-start.3 = (bf16[256,2048]{1,0:T(8,128)(2,1)S(1)}, bf16[256,2048]{1,0:T(8,128)(2,1)}, u32[]{:S(2)}) copy-start(bf16[256,2048]{1,0:T(8,128)(2,1)} %k_ref.3) | copy-start | bytes 3145732
  2.6 1.2 %copy-start.5 = (bf16[256,2048]{1,0:T(8,128)(2,1)S(1)}, bf16[256,2048]{1,0:T(8,128)(2,1)}, u32[]{:S(2)}) copy-start(bf16[256,2048]{1,0:T(8,128)(2,1)} %v_ref.3) | copy-start | bytes 3145732
  3.8 1.2 %copy-start.7 = (bf16[256,2048]{1,0:T(8,128)(2,1)S(1)}, bf16[256,2048]{1,0:T(8,128)(2,1)}, u32[]{:S(2)}) copy-start(bf16[256,2048]{1,0:T(8,128)(2,1)} %w_ref.3) | copy-start | bytes 3145732
  5.1 15.5 %copy-start.10 = (f32[16,64]{1,0:T(8,128)S(1)}, f32[16,64]{1,0:T(8,128)}, u32[]{:S(2)}) copy-start(f32[16,64]{1,0:T(8,128)} %param.13) | copy-start | bytes 12292
  5.1 15.6 %copy-start.9 = (f32[1024]{0:T(1024)S(1)}, f32[1024]{0:T(1024)}, u32[]{:S(2)}) copy-start(f32[1024]{0:T(1024)} %param.14) | copy-start | bytes 12292
  10.4 23.8 %all-to-all-start = ((bf16[128,16,128]{2,1,0:T(8,128)(2,1)}), bf16[128,16,128]{2,1,0:T(8,128)(2,1)S(1)}, u32[]{:S(2)}, u32[]{:S(2)}) async-start(bf16[128,16,128]{2,1,0:T(8,128)(2,1)} %state.1), calls=%async_computation | async-start | bytes 1048576 | tf_op jit(solution)/shard_map/all_to_all | solution.py:207
  20.7 2.0 %collective-permute-start = (f32[2,1024]{1,0:T(2,128)S(1)}, f32[2,1024]{1,0:T(2,128)S(1)}, u32[]{:S(2)}, u32[]{:S(2)}) collective-permute-start(f32[2,1024]{1,0:T(2,128)S(1)} %pad_maximum_fusion.1), channel_id=1, source_target_pairs={{0,1},{1,0},{2,3},{3,2},{4,5},{5,4},{6,7},{7,6},{8,9},{9,8},{10,11... | collective-permute-start | bytes 24584 | tf_op jit(solution)/shard_map/ppermute | solution.py:189
  35.2 16.7 %all-to-all-start.1 = ((bf16[128,8,128]{2,1,0:T(8,128)(2,1)}), bf16[128,8,128]{2,1,0:T(8,128)(2,1)S(1)}, u32[]{:S(2)}, u32[]{:S(2)}) async-start(bf16[128,8,128]{2,1,0:T(8,128)(2,1)} %scan.1), calls=%async_computation.1 | async-start | bytes 524288 | tf_op jit(solution)/shard_map/all_to_all | solution.py:235
  39.8 1.2 %copy-start.4 = (bf16[256,2048]{1,0:T(8,128)(2,1)S(1)}, bf16[256,2048]{1,0:T(8,128)(2,1)}, u32[]{:S(2)}) copy-start(bf16[256,2048]{1,0:T(8,128)(2,1)} %k_ref.3) | copy-start | bytes 3145732
  41.0 1.2 %copy-start.6 = (bf16[256,2048]{1,0:T(8,128)(2,1)S(1)}, bf16[256,2048]{1,0:T(8,128)(2,1)}, u32[]{:S(2)}) copy-start(bf16[256,2048]{1,0:T(8,128)(2,1)} %v_ref.3) | copy-start | bytes 3145732
  42.3 1.2 %copy-start.8 = (bf16[256,2048]{1,0:T(8,128)(2,1)S(1)}, bf16[256,2048]{1,0:T(8,128)(2,1)}, u32[]{:S(2)}) copy-start(bf16[256,2048]{1,0:T(8,128)(2,1)} %w_ref.3) | copy-start | bytes 3145732
  43.5 8.4 %copy-start.1 = (bf16[256,2048]{1,0:T(8,128)(2,1)S(1)}, bf16[256,2048]{1,0:T(8,128)(2,1)}, u32[]{:S(2)}) copy-start(bf16[256,2048]{1,0:T(8,128)(2,1)} %g_ref.1) | copy-start | bytes 3145732
  51.9 1.6 %copy-start = (f32[256,2048]{1,0:T(8,128)S(1)}, f32[256,2048]{1,0:T(8,128)}, u32[]{:S(2)}) copy-start(f32[256,2048]{1,0:T(8,128)} %get-tuple-element.7.out_ref) | copy-start | bytes 6291460
where the time goes:
time: 71.7 us; the launch traced here: 71.1 us
  Pallas kernels  32.3 us (45%)
  starting transfers between devices  17.3 us (24%)
  waiting for transfers between devices  12.3 us (17%)
  local copies, waits for them, and re-layouts  9.02 us (13%)
    pallas_call x1, Pallas kernels, shards(): pl.pallas_call(finish_kernel, grid_spec=pltpu.PrefetchScalarGridSpec(num_...  17.6 us
    all_to_all x1, waiting for transfers between devices, shards(): msg = lax.all_to_all(msg, SEQ_HEAD, split_axis=0, concat_axis=0, tiled=True)  11.5 us
    all_to_all x1, starting transfers between devices, shards(): msg = lax.all_to_all(msg, SEQ_HEAD, split_axis=0, concat_axis=0, tiled=True)  10.2 us
    unnamed x22, local copies, waits for them, and re-layouts  8.94 us
    pallas_call x1, Pallas kernels, local(): pl.pallas_call(local_kernel, grid=(count,), in_specs=[blk] * 4 + [pl.Bloc...  8.42 us
    pallas_call x1, Pallas kernels, shards(): pl.pallas_call(state_kernel, grid=(chunks,), in_specs=[block] * 3, out_sp...  5.29 us
    all_to_all x1, starting transfers between devices, shards(): lax.all_to_all(entering, SEQ_HEAD, split_axis=0, concat_axis=0, tiled=True)  4.6 us
  transfers between devices with their start and end apart: 4, of which 2 were waited for; matrix products, arithmetic and copies ran while one was open for 0% of the time, Pallas kernels for 21%

commit v1 on v0

v1 whole, which is shorter than its diff:
```python
import functools

import jax
import jax.numpy as jnp
from jax import lax
from jax.experimental import pallas as pl
from jax.experimental.pallas import tpu as pltpu
from jax.sharding import Mesh
from jax.sharding import PartitionSpec as P

BLOCK = 128
HALF = 64
PAIR = 128
WIDE = 256
SEQ_HEAD = ("seq_0", "seq_1", "seq_2", "head")
EPS = 1e-05
BF = jnp.bfloat16
F32 = jnp.float32


def mm(a, b):
    return lax.dot_general(a, b, (((1,), (0,)), ((), ())), preferred_element_type=F32)


def mm_nt(a, b):
    return lax.dot_general(a, b, (((1,), (1,)), ((), ())), preferred_element_type=F32)


def mm_tn(a, b):
    return lax.dot_general(a, b, (((0,), (0,)), ((), ())), preferred_element_type=F32)


def grid2(rows, cols):
    return (
        lax.broadcasted_iota(jnp.int32, (rows, cols), 0),
        lax.broadcasted_iota(jnp.int32, (rows, cols), 1),
    )


def two_parts(x):
    hi = x.astype(BF)
    return hi, (x - hi.astype(F32)).astype(BF)


def head_ones(scale):
    row, col = grid2(WIDE, WIDE)
    return jnp.where(row // HALF == col // HALF, scale, 0.0).astype(BF)


def centred(v):
    return (v.astype(F32) - mm(v, head_ones(1.0 / HALF))).astype(BF)


def state_kernel(k_hbm, v_hbm, w_hbm, msg_hbm, k_buf, v_buf, w_buf, msg_buf, in_sems, out_sems):
    tokens, width = k_buf.shape
    chunks = in_sems.shape[1]
    wide = width // chunks
    per = msg_buf.shape[0] // chunks
    loads = [
        [
            pltpu.make_async_copy(
                src.at[:, pl.ds(i * wide, wide)], dst.at[:, pl.ds(i * wide, wide)], in_sems.at[j, i]
            )
            for j, (src, dst) in enumerate(((w_hbm, w_buf), (k_hbm, k_buf), (v_hbm, v_buf)))
        ]
        for i in range(chunks)
    ]
    stores = [
        pltpu.make_async_copy(
            msg_buf.at[pl.ds(i * per, per)], msg_hbm.at[pl.ds(i * per, per)], out_sems.at[i]
        )
        for i in range(chunks)
    ]
    for chunk in loads:
        for one in chunk:
            one.start()
    row, col = grid2(tokens, tokens)
    later = jnp.where(col > row, 1.0, 0.0).astype(BF)
    first = lax.broadcasted_iota(jnp.int32, (HALF, PAIR), 1) < HALF
    for i in range(chunks):
        for one in loads[i]:
            one.wait()
        for part in range(i * wide // WIDE, (i + 1) * wide // WIDE):
            s = slice(part * WIDE, (part + 1) * WIDE)
            log_decay = -jnp.exp(w_buf[:, s].astype(F32))
            hi, lo = two_parts(log_decay)
            after = mm(later, hi) + mm(later, lo)
            key_end = (k_buf[:, s].astype(F32) * jnp.exp(after)).astype(BF)
            total = after[0:1] + log_decay[0:1]
            state = mm_tn(v_buf[:, s], key_end)
            tot_hi, tot_lo = two_parts(total)
            logs = jnp.concatenate([tot_hi, tot_lo], axis=0)
            for p in range(WIDE // PAIR):
                at = p * PAIR
                both = jnp.where(
                    first,
                    state[at : at + HALF, at : at + PAIR],
                    state[at + HALF : at + PAIR, at : at + PAIR],
                )
                both = (both - jnp.mean(both, axis=0, keepdims=True)).astype(BF)
                base = (part * (WIDE // PAIR) + p) * 8
                msg_buf[base : base + 8, 0:4] = both.reshape(8, 4, 2, PAIR)
                msg_buf[base : base + 8, 4] = jnp.broadcast_to(
                    logs[None, :, at : at + PAIR], (8, 2, PAIR)
                )
        stores[i].start()
    for one in stores:
        one.wait()


def local_kernel(
    r_ref, k_ref, v_ref, w_ref, g_ref, u_ref, gain_ref, out_ref, rin_ref, sg_ref
):
    tokens = r_ref.shape[0]
    row, col = grid2(tokens, tokens)
    upto = jnp.where(col <= row, 1.0, 0.0).astype(BF)
    lane = lax.broadcasted_iota(jnp.int32, (BLOCK, PAIR), 1)
    first = lane < HALF
    zero = jnp.zeros((BLOCK, PAIR), BF)
    row, col = grid2(BLOCK, BLOCK)
    strict = row > col

    def stacked(x):
        return jnp.concatenate([jnp.where(first, x, zero), jnp.where(first, zero, x)], axis=0)

    def side(scores, masked):
        a, b = scores[:BLOCK], scores[BLOCK:]
        if masked:
            a, b = jnp.where(strict, a, 0.0), jnp.where(strict, b, 0.0)
        return jnp.concatenate([a, b], axis=1).astype(BF)

    for part in range(r_ref.shape[1] // WIDE):
        at = part * WIDE
        c = slice(at, at + WIDE)
        gate = g_ref[:, c].astype(F32)
        sg_ref[:, c] = (0.5 * gate * (1.0 + jnp.tanh(0.5 * gate)) * gain_ref[:, c]).astype(BF)
        log_decay = -jnp.exp(w_ref[:, c].astype(F32))
        hi, lo = two_parts(log_decay)
        cum = mm(upto, hi) + mm(upto, lo)
        before = cum - log_decay
        r = r_ref[:, c].astype(F32)
        k = k_ref[:, c].astype(F32)
        v = centred(v_ref[:, c])
        mid0, end0, mid1 = cum[63:64], cum[127:128], cum[191:192]
        r0 = r[:BLOCK] * jnp.exp(before[:BLOCK] - mid0)
        k0 = k[:BLOCK] * jnp.exp(mid0 - cum[:BLOCK])
        r1 = r[BLOCK:] * jnp.exp(before[BLOCK:] - mid1)
        k1 = k[BLOCK:] * jnp.exp(mid1 - cum[BLOCK:])
        r1c = r1 * jnp.exp(mid1 - end0)
        k0c = k0 * jnp.exp(end0 - mid0)
        rin_ref[:BLOCK, c] = (r0 * jnp.exp(mid0)).astype(BF)
        rin_ref[BLOCK:, c] = (r1c * jnp.exp(end0)).astype(BF)
        own = mm((r * u_ref[:, c] * k).astype(BF), head_ones(1.0)) * v.astype(F32)
        r0, k0, r1, k1, r1c, k0c = (x.astype(BF) for x in (r0, k0, r1, k1, r1c, k0c))
        for p in range(WIDE // PAIR):
            s = slice(p * PAIR, (p + 1) * PAIR)
            o = slice(at + p * PAIR, at + (p + 1) * PAIR)
            s00 = side(mm_nt(stacked(r0[:, s]), k0[:, s]), True)
            s10 = side(mm_nt(stacked(r1c[:, s]), k0c[:, s]), False)
            s11 = side(mm_nt(stacked(r1[:, s]), k1[:, s]), True)
            v0, v1 = stacked(v[:BLOCK, s]), stacked(v[BLOCK:, s])
            out_ref[:BLOCK, o] = mm(s00, v0) + own[:BLOCK, s]
            out_ref[BLOCK:, o] = mm(s10, v0) + mm(s11, v1) + own[BLOCK:, s]


def scan_kernel(msg_ref, after_ref, out_ref):
    groups = msg_ref.shape[0]
    state = jnp.zeros((8, PAIR), F32)
    for g in range(groups):
        logs = msg_ref[g, 4].astype(F32)
        out_ref[g] = state.astype(BF)
        decay = jnp.exp(logs[0:1] + logs[1:2])
        state = state * decay + msg_ref[g, 0:4].reshape(8, PAIR).astype(F32)


def finish_kernel(
    c_ref,
    s_hbm,
    out_hbm,
    rin_hbm,
    sg_hbm,
    w1_hbm,
    w2_hbm,
    y_hbm,
    s_ref,
    out_buf,
    rin_buf,
    sg_buf,
    w_buf,
    gated,
    y_buf,
    s_sem,
    in_sems,
    w_sems,
    y_sems,
):
    chunks = in_sems.shape[1]
    tiles = y_sems.shape[0]
    wide = out_buf.shape[1] // chunks
    tile = y_buf.shape[1] // tiles
    half = out_buf.shape[1] // 2
    loads = [
        [
            pltpu.make_async_copy(
                src.at[:, pl.ds(i * wide, wide)], dst.at[:, pl.ds(i * wide, wide)], in_sems.at[j, i]
            )
            for j, (src, dst) in enumerate(((out_hbm, out_buf), (rin_hbm, rin_buf), (sg_hbm, sg_buf)))
        ]
        for i in range(chunks)
    ]

    def cols(t):
        return pl.ds(pl.multiple_of(t * tile, tile), tile)

    def fetch(j, t):
        src = (w1_hbm, w2_hbm)[j]
        return pltpu.make_async_copy(src.at[:, cols(t)], w_buf.at[j, :, cols(t)], w_sems.at[j, t])

    def store(t):
        return pltpu.make_async_copy(y_buf.at[:, cols(t)], y_hbm.at[:, cols(t)], y_sems.at[t])

    entering_load = pltpu.make_async_copy(s_hbm, s_ref, s_sem)
    entering_load.start()
    for chunk in loads:
        for one in chunk:
            one.start()
    entering_load.wait()
    first = lax.broadcasted_iota(jnp.int32, (HALF, PAIR), 1) < HALF
    zero = jnp.zeros((HALF, PAIR), BF)
    share = head_ones(1.0 / HALF)
    for i in range(chunks):
        for one in loads[i]:
            one.wait()
        fetch(0, i).start()
        fetch(1, i).start()
        for part in range(i * wide // WIDE, (i + 1) * wide // WIDE):
            c = slice(part * WIDE, (part + 1) * WIDE)
            a, b = s_ref[2 * part], s_ref[2 * part + 1]
            entering = jnp.concatenate(
                [
                    jnp.concatenate([jnp.where(first, a, zero), zero], axis=1),
                    jnp.concatenate([jnp.where(first, zero, a), zero], axis=1),
                    jnp.concatenate([zero, jnp.where(first, b, zero)], axis=1),
                    jnp.concatenate([zero, jnp.where(first, zero, b)], axis=1),
                ],
                axis=0,
            )
            wkv = out_buf[:, c] + mm_nt(rin_buf[:, c], entering)
            var = mm((wkv * wkv).astype(BF), share)
            to = part * WIDE % half
            gated[part * WIDE // half, :, to : to + WIDE] = (
                wkv * lax.rsqrt(var + EPS) * sg_buf[:, c].astype(F32)
            ).astype(BF)

    mine = c_ref[0]

    def project(t, carry):
        fetch(0, t).wait()
        fetch(1, t).wait()

        @pl.when(t + chunks < tiles)
        def _():
            fetch(0, t + chunks).start()
            fetch(1, t + chunks).start()

        y = mm(gated[mine], w_buf[0, :, cols(t)]) + mm(gated[1 - mine], w_buf[1, :, cols(t)])
        y_buf[:, cols(t)] = y.astype(BF)
        store(t).start()
        return carry

    lax.fori_loop(0, tiles, project, 0)
    for t in range(tiles):
        store(t).wait()


def params(*semantics, limit=66_000_000):
    return pltpu.CompilerParams(dimension_semantics=semantics, vmem_limit_bytes=limit)


def call_state(k, v, w, groups):
    chunks = 4
    any_block = pl.BlockSpec(memory_space=pl.ANY)
    shape = (groups, 5, 2, PAIR)
    return pl.pallas_call(
        state_kernel,
        in_specs=[any_block] * 3,
        out_specs=any_block,
        out_shape=jax.ShapeDtypeStruct(shape, BF),
        scratch_shapes=[pltpu.VMEM(k.shape, BF)] * 3
        + [
            pltpu.VMEM(shape, BF),
            pltpu.SemaphoreType.DMA((3, chunks)),
            pltpu.SemaphoreType.DMA((chunks,)),
        ],
        compiler_params=params(),
        cost_estimate=pl.CostEstimate(flops=4 << 30, bytes_accessed=4 << 20, transcendentals=1 << 20),
        name="state",
    )(k, v, w)


def call_local(r, k, v, w, g, bonus, gain, start, count):
    tokens = r.shape[0]
    wide = 2 * WIDE
    blk = pl.BlockSpec((tokens, wide), lambda i: (0, i + start))
    row = pl.BlockSpec((1, wide), lambda i: (0, i + start))
    out_blk = pl.BlockSpec((tokens, wide), lambda i: (0, i))
    return pl.pallas_call(
        local_kernel,
        grid=(count,),
        in_specs=[blk] * 5 + [row] * 2,
        out_specs=[out_blk] * 3,
        out_shape=[jax.ShapeDtypeStruct((tokens, count * wide), t) for t in (F32, BF, BF)],
        compiler_params=params("arbitrary"),
        cost_estimate=pl.CostEstimate(flops=4 << 30, bytes_accessed=10 << 20, transcendentals=4 << 20),
        name="local",
    )(r, k, v, w, g, bonus, gain)


def call_scan(msg, anchor):
    anchor = pltpu.with_memory_space_constraint(anchor, pltpu.HBM)
    return pl.pallas_call(
        scan_kernel,
        in_specs=[pl.BlockSpec(memory_space=pltpu.VMEM), pl.BlockSpec(memory_space=pl.ANY)],
        out_shape=jax.ShapeDtypeStruct((msg.shape[0], 8, PAIR), BF),
        compiler_params=params(limit=8 << 20),
        name="scan",
    )(msg, anchor)


def call_finish(core, out, rin, entering, sg, weight, other_weight):
    tokens, width = out.shape
    cols = weight.shape[1]
    chunks, tiles = 4, 8
    any_block = pl.BlockSpec(memory_space=pl.ANY)
    return pl.pallas_call(
        finish_kernel,
        in_specs=[
            pl.BlockSpec(memory_space=pltpu.SMEM),
        ]
        + [any_block] * 6,
        out_specs=any_block,
        out_shape=jax.ShapeDtypeStruct((tokens, cols), BF),
        scratch_shapes=[
            pltpu.VMEM(entering.shape, BF),
            pltpu.VMEM(out.shape, F32),
            pltpu.VMEM(out.shape, BF),
            pltpu.VMEM(out.shape, BF),
            pltpu.VMEM((2, width // 2, cols), BF),
            pltpu.VMEM((2, tokens, width // 2), BF),
            pltpu.VMEM((tokens, cols), BF),
            pltpu.SemaphoreType.DMA,
            pltpu.SemaphoreType.DMA((3, chunks)),
            pltpu.SemaphoreType.DMA((2, tiles)),
            pltpu.SemaphoreType.DMA((tiles,)),
        ],
        compiler_params=params(limit=58 << 20),
        name="finish",
    )(core.reshape(1).astype(jnp.int32), entering, out, rin, sg, weight, other_weight)


def shards(r, k, v, w, g, bonus, gain, weight):
    groups = lax.axis_size(SEQ_HEAD)
    core = lax.axis_index("head")
    r, k, v, w, g = (pltpu.with_memory_space_constraint(x, pltpu.HBM) for x in (r, k, v, w, g))
    swap = [(0, 1), (1, 0)]
    other_weight = lax.ppermute(weight, "head", swap)
    small = jnp.stack([bonus.reshape(-1), gain])
    other_small = lax.ppermute(small, "head", swap)
    low = jnp.where(core == 0, small, other_small)
    high = jnp.where(core == 0, other_small, small)
    small = jnp.concatenate([low, high], axis=1)
    bonus, gain = small[0:1], small[1:2]
    msg = call_state(k, v, w, groups)
    msg = lax.all_to_all(msg, SEQ_HEAD, split_axis=0, concat_axis=0, tiled=True)
    out, rin, sg = call_local(r, k, v, w, g, bonus, gain, 0, r.shape[1] // (2 * WIDE))
    entering = call_scan(msg, rin)
    entering = lax.all_to_all(entering, SEQ_HEAD, split_axis=0, concat_axis=0, tiled=True)
    entering = entering.reshape(-1, HALF, PAIR)
    return call_finish(core, out, rin, entering, sg, weight, other_weight)


def solution(mesh):
    torus = Mesh(mesh.devices.reshape(4, 4, 4, mesh.shape["head"]), SEQ_HEAD)
    in_specs = (P(SEQ_HEAD, None),) * 5 + (P("head", None), P("head"), P("head", None))
    return jax.shard_map(
        shards, mesh=torus, in_specs=in_specs, out_specs=P(SEQ_HEAD, None), check_vma=False
    )
```

time: 71.7 us -> 60.9 us (0.85)
  blocking collectives: 0 us -> 18.7 us
  waiting for transfers between devices: 12.3 us -> 2.1 us
  local copies, waits for them, and re-layouts: 9.02 us -> 0.78 us
  Pallas kernels: 32.3 us -> 25.6 us
  starting transfers between devices: 17.3 us -> 12.1 us
  other arithmetic: 0.04 us -> 1.33 us
    all_to_all x0 -> x1, blocking collectives: none -> 18.7 us  [shards(): lax.all_to_all(entering, SEQ_HEAD, split_axis=0, concat_axis=0, tiled=True)]
    all_to_all x1, waiting for transfers between devices: 11.5 us -> 2.1 us  [shards(): msg = lax.all_to_all(msg, SEQ_HEAD, split_axis=0, concat_axis=0, tiled=True)]
    unnamed x22 -> x2, local copies, waits for them, and re-layouts: 8.94 us -> 0.01 us
    pallas_call x4, Pallas kernels: 32.3 us -> 25.6 us  [the longest x1 10.9 us: call_finish(): pl.pallas_call(finish_kernel, in_specs=[pl.BlockSpec(memory_space=pltpu.S...]
    all_to_all x1 -> x0, starting transfers between devices: 4.6 us -> none  [shards(): lax.all_to_all(entering, SEQ_HEAD, split_axis=0, concat_axis=0, tiled=True)]
    ppermute x1, starting transfers between devices: 1.15 us -> 0.09 us  [shards(): other_small = lax.ppermute(small, 'head', swap)]
    ppermute x1, waiting for transfers between devices: 0.83 us -> 0.01 us  [shards(): other_small = lax.ppermute(small, 'head', swap)]
  transfers between devices with their start and end apart: 4 -> 3, of which waited for: 2 -> 1; matrix products, arithmetic and copies ran while one was open for 0% -> 3% of each run, Pallas kernels for 21% -> 24%
where the time goes in v1:
time: 60.9 us; the launch traced here: 60.6 us
  Pallas kernels  25.6 us (42%)
  blocking collectives  18.7 us (31%)
  starting transfers between devices  12.1 us (20%)
  waiting for transfers between devices  2.1 us (3%)
  other arithmetic  1.33 us (2%)
  local copies, waits for them, and re-layouts  0.78 us (1%)
    all_to_all x1, blocking collectives, shards(): lax.all_to_all(entering, SEQ_HEAD, split_axis=0, concat_axis=0, tiled=True)  18.7 us
    pallas_call x1, Pallas kernels, call_finish(): pl.pallas_call(finish_kernel, in_specs=[pl.BlockSpec(memory_space=pltpu.S...  10.9 us
    all_to_all x1, starting transfers between devices, shards(): msg = lax.all_to_all(msg, SEQ_HEAD, split_axis=0, concat_axis=0, tiled=True)  10.6 us
    pallas_call x1, Pallas kernels, call_local(): pl.pallas_call(local_kernel, grid=(count,), in_specs=[blk] * 5 + [row] *...  9.01 us
    pallas_call x1, Pallas kernels, call_state(): pl.pallas_call(state_kernel, in_specs=[any_block] * 3, out_specs=any_bloc...  5.38 us
    all_to_all x1, waiting for transfers between devices, shards(): msg = lax.all_to_all(msg, SEQ_HEAD, split_axis=0, concat_axis=0, tiled=True)  2.1 us
    ppermute x1, starting transfers between devices, shards(): other_weight = lax.ppermute(weight, 'head', swap)  1.38 us
  transfers between devices with their start and end apart: 3, of which 1 were waited for; matrix products, arithmetic and copies ran while one was open for 3% of the time, Pallas kernels for 24%

profile of v1, /device:TPU:1, one launch (start us, length us, event | category | flops | bytes accessed | tf_op | source)
XLA Modules:
  0.0 60.6 jit_solution(8130564980682538088)
XLA Ops:
  0.0 0.0 copy-start
  0.0 1.4 %collective-permute-start.1 = (bf16[1024,4096]{1,0:T(8,128)(2,1)}, bf16[1024,4096]{1,0:T(8,128)(2,1)}, u32[]{:S(2)}, u32[]{:S(2)}) collective-permute-start(bf16[1024,4096]{1,0:T(8,128)(2,1)} %w1_hbm.1), channel_id=1, source_target_pairs={{0,1},{1,0},{2,3},{3,2},{4,5},{5,4},{6,7},{7,6},{8,9},{9,8},{10,11... | collective-permute-start | bytes 25165832 | tf_op jit(solution)/shard_map/ppermute | solution.py:366
  1.4 0.8 %stack_reshape.3 = f32[1,1024]{1,0:T(1,128)S(1)} reshape(f32[16,64]{1,0:T(8,128)} %param.13) | data formatting | bytes 8192 | tf_op jit(solution)/shard_map/stack;reshape | solution.py:367
  2.2 0.7 %pad_maximum_fusion.1 = f32[2,1024]{1,0:T(2,128)S(1)} fusion(f32[1,1024]{1,0:T(1,128)} %bitcast.4, f32[1,1024]{1,0:T(1,128)S(1)} %stack_reshape.3), kind=kLoop, calls=%fused_computation.4 | loop fusion | flops 2048 | bytes 16384 | tf_op jit(solution)/shard_map/stack | solution.py:367
  2.9 0.1 collective-permute-start
  3.0 5.4 %state.1 = bf16[128,5,2,128]{3,2,1,0:T(2,128)(2,1)} custom-call(bf16[256,2048]{1,0:T(8,128)(2,1)} %k_ref.1, bf16[256,2048]{1,0:T(8,128)(2,1)} %v_ref.1, bf16[256,2048]{1,0:T(8,128)(2,1)} %w_ref.1), custom_call_target="tpu_custom_call" | custom-call | flops 4294967296 | bytes 4194304 | tf_op jit(solution)/shard_map/state/pallas_call | solution.py:284
  8.3 10.6 %all-to-all-start = ((bf16[128,5,2,128]{3,2,1,0:T(2,128)(2,1)}), bf16[128,5,2,128]{3,2,1,0:T(2,128)(2,1)S(1)}, u32[]{:S(2)}, u32[]{:S(2)}) async-start(bf16[128,5,2,128]{3,2,1,0:T(2,128)(2,1)} %state.1), calls=%async_computation | async-start | bytes 655360 | tf_op jit(solution)/shard_map/all_to_all | solution.py:374
  19.0 0.0 collective-permute-done
  19.0 0.0 copy-done
  19.0 0.6 %pad_maximum_fusion = (f32[1,2048]{1,0:T(1,128)}, f32[1,2048]{1,0:T(1,128)}) fusion(f32[2,1024]{1,0:T(2,128)S(1)} %get-tuple-element.13, f32[2,1024]{1,0:T(2,128)S(1)} %get-tuple-element.14), kind=kLoop, calls=%fused_computation.3 | loop fusion | flops 4096 | bytes 32768 | tf_op jit(solution)/shard_map/concatenate | solution.py:371
  19.6 9.0 %local.1 = (f32[256,2048]{1,0:T(8,128)}, bf16[256,2048]{1,0:T(8,128)(2,1)}, bf16[256,2048]{1,0:T(8,128)(2,1)}) custom-call(bf16[256,2048]{1,0:T(8,128)(2,1)} %r_ref.1, bf16[256,2048]{1,0:T(8,128)(2,1)} %k_ref.1, bf16[256,2048]{1,0:T(8,128)(2,1)} %v_ref.1, bf16[256,2048]{1,0:T(8,128)(2,1)} %w_ref.1, bf16[256,2048]{1,0:T(8,128)(2,1)} %g_ref.1, ...), custom_call_target="tpu_custom_call" | custom-call | flops 4294967296 | bytes 10485760 | tf_op jit(solution)/shard_map/local/pallas_call | solution.py:307
  28.6 2.1 %all-to-all-done.msg_ref = bf16[128,5,2,128]{3,2,1,0:T(2,128)(2,1)S(1)} async-done(((bf16[128,5,2,128]{3,2,1,0:T(2,128)(2,1)}), bf16[128,5,2,128]{3,2,1,0:T(2,128)(2,1)S(1)}, u32[]{:S(2)}, u32[]{:S(2)}) %all-to-all-start) | async-done | bytes 327712 | tf_op jit(solution)/shard_map/all_to_all | solution.py:374
  30.7 0.3 scan.1
  31.0 18.7 %all_to_all.10 = bf16[128,8,128]{2,1,0:T(8,128)(2,1)} all-to-all(bf16[128,8,128]{2,1,0:T(8,128)(2,1)S(1)} %scan.1), channel_id=1, replica_groups=mesh['seq_0'=4,'seq_1'=4,'seq_2'=4,'head'=2] {'seq_0','seq_1','seq_2','h..., dimensions={0} | all-to-all | bytes 524288 | tf_op jit(solution)/shard_map/all_to_all | solution.py:377
  49.7 0.0 collective-permute-done.1.w2_hbm
  49.7 10.9 %finish.1 = bf16[256,4096]{1,0:T(8,128)(2,1)} custom-call(s32[1]{0:T(128)} %bitcast.c_ref, bf16[16,64,128]{2,1,0:T(8,128)(2,1)} %bitcast.3, f32[256,2048]{1,0:T(8,128)} %get-tuple-element.9.out_hbm, bf16[256,2048]{1,0:T(8,128)(2,1)} %get-tuple-element.8.after_ref.rin_hbm, bf16[256,2048]{1,0:T(8,128)(2,1)} %get-tuple-element.10.sg_hbm, ...), custom_call_target="tpu_custom_call" | custom-call | tf_op jit(solution)/shard_map/finish/pallas_call | solution.py:335
  (1 shorter events, 0.0 us)
Async XLA Ops:
  0.0 19.0 %copy-start = (f32[1024]{0:T(1024)S(1)}, f32[1024]{0:T(1024)}, u32[]{:S(2)}) copy-start(f32[1024]{0:T(1024)} %param.14) | copy-start | bytes 12292
  0.0 49.7 %collective-permute-start.1 = (bf16[1024,4096]{1,0:T(8,128)(2,1)}, bf16[1024,4096]{1,0:T(8,128)(2,1)}, u32[]{:S(2)}, u32[]{:S(2)}) collective-permute-start(bf16[1024,4096]{1,0:T(8,128)(2,1)} %w1_hbm.1), channel_id=1, source_target_pairs={{0,1},{1,0},{2,3},{3,2},{4,5},{5,4},{6,7},{7,6},{8,9},{9,8},{10,11... | collective-permute-start | bytes 25165832 | tf_op jit(solution)/shard_map/ppermute | solution.py:366
  2.9 16.1 %collective-permute-start = (f32[2,1024]{1,0:T(2,128)S(1)}, f32[2,1024]{1,0:T(2,128)S(1)}, u32[]{:S(2)}, u32[]{:S(2)}) collective-permute-start(f32[2,1024]{1,0:T(2,128)S(1)} %pad_maximum_fusion.1), channel_id=1, source_target_pairs={{0,1},{1,0},{2,3},{3,2},{4,5},{5,4},{6,7},{7,6},{8,9},{9,8},{10,11... | collective-permute-start | bytes 24584 | tf_op jit(solution)/shard_map/ppermute | solution.py:368
  8.3 22.4 %all-to-all-start = ((bf16[128,5,2,128]{3,2,1,0:T(2,128)(2,1)}), bf16[128,5,2,128]{3,2,1,0:T(2,128)(2,1)S(1)}, u32[]{:S(2)}, u32[]{:S(2)}) async-start(bf16[128,5,2,128]{3,2,1,0:T(2,128)(2,1)} %state.1), calls=%async_computation | async-start | bytes 655360 | tf_op jit(solution)/shard_map/all_to_all | solution.py:374

commit v2 on v1

--- a/solution.py
+++ b/solution.py
@@ -14,6 +14,10 @@
 WIDE = 256
 SEQ_HEAD = ("seq_0", "seq_1", "seq_2", "head")
 EPS = 1e-05
+LOG2E = 1.4426950408889634
+LOG2LOG2E = 0.5287663729448977
+WEIGHT_STAGES = ((0, 1), (2, 3), (4,), (5,))
+WEIGHTS_AHEAD = 6
 BF = jnp.bfloat16
 F32 = jnp.float32
 
@@ -45,6 +49,10 @@
 def head_ones(scale):
     row, col = grid2(WIDE, WIDE)
     return jnp.where(row // HALF == col // HALF, scale, 0.0).astype(BF)
+
+
+def decay_rate(w):
+    return jnp.exp2(w.astype(F32) * LOG2E + LOG2LOG2E).astype(BF)
 
 
 def centred(v):
@@ -71,22 +79,24 @@
         )
         for i in range(chunks)
     ]
-    for chunk in loads:
+    depth = chunks
+    for chunk in loads[:depth]:
         for one in chunk:
             one.start()
     row, col = grid2(tokens, tokens)
-    later = jnp.where(col > row, 1.0, 0.0).astype(BF)
+    later = jnp.where(col > row, -1.0, 0.0).astype(BF)
     first = lax.broadcasted_iota(jnp.int32, (HALF, PAIR), 1) < HALF
     for i in range(chunks):
         for one in loads[i]:
             one.wait()
+        for one in loads[i + depth] if i + depth < chunks else ():
+            one.start()
         for part in range(i * wide // WIDE, (i + 1) * wide // WIDE):
             s = slice(part * WIDE, (part + 1) * WIDE)
-            log_decay = -jnp.exp(w_buf[:, s].astype(F32))
-            hi, lo = two_parts(log_decay)
-            after = mm(later, hi) + mm(later, lo)
-            key_end = (k_buf[:, s].astype(F32) * jnp.exp(after)).astype(BF)
-            total = after[0:1] + log_decay[0:1]
+            rate = decay_rate(w_buf[:, s])
+            after = mm(later, rate)
+            key_end = k_buf[:, s] * jnp.exp2(after).astype(BF)
+            total = after[0:1] - rate[0:1].astype(F32)
             state = mm_tn(v_buf[:, s], key_end)
             tot_hi, tot_lo = two_parts(total)
             logs = jnp.concatenate([tot_hi, tot_lo], axis=0)
@@ -113,7 +123,8 @@
 ):
     tokens = r_ref.shape[0]
     row, col = grid2(tokens, tokens)
-    upto = jnp.where(col <= row, 1.0, 0.0).astype(BF)
+    upto = jnp.where(col <= row, -1.0, 0.0).astype(BF)
+    prior = jnp.where(col < row, -1.0, 0.0).astype(BF)
     lane = lax.broadcasted_iota(jnp.int32, (BLOCK, PAIR), 1)
     first = lane < HALF
     zero = jnp.zeros((BLOCK, PAIR), BF)
@@ -134,24 +145,23 @@
         c = slice(at, at + WIDE)
         gate = g_ref[:, c].astype(F32)
         sg_ref[:, c] = (0.5 * gate * (1.0 + jnp.tanh(0.5 * gate)) * gain_ref[:, c]).astype(BF)
-        log_decay = -jnp.exp(w_ref[:, c].astype(F32))
-        hi, lo = two_parts(log_decay)
-        cum = mm(upto, hi) + mm(upto, lo)
-        before = cum - log_decay
-        r = r_ref[:, c].astype(F32)
-        k = k_ref[:, c].astype(F32)
+        rate = decay_rate(w_ref[:, c])
+        cum = mm(upto, rate)
+        before = mm(prior, rate)
+        r = r_ref[:, c]
+        k = k_ref[:, c]
         v = centred(v_ref[:, c])
         mid0, end0, mid1 = cum[63:64], cum[127:128], cum[191:192]
-        r0 = r[:BLOCK] * jnp.exp(before[:BLOCK] - mid0)
-        k0 = k[:BLOCK] * jnp.exp(mid0 - cum[:BLOCK])
-        r1 = r[BLOCK:] * jnp.exp(before[BLOCK:] - mid1)
-        k1 = k[BLOCK:] * jnp.exp(mid1 - cum[BLOCK:])
-        r1c = r1 * jnp.exp(mid1 - end0)
-        k0c = k0 * jnp.exp(end0 - mid0)
-        rin_ref[:BLOCK, c] = (r0 * jnp.exp(mid0)).astype(BF)
-        rin_ref[BLOCK:, c] = (r1c * jnp.exp(end0)).astype(BF)
-        own = mm((r * u_ref[:, c] * k).astype(BF), head_ones(1.0)) * v.astype(F32)
-        r0, k0, r1, k1, r1c, k0c = (x.astype(BF) for x in (r0, k0, r1, k1, r1c, k0c))
+        r0 = r[:BLOCK] * jnp.exp2(before[:BLOCK] - mid0).astype(BF)
+        k0 = k[:BLOCK] * jnp.exp2(mid0 - cum[:BLOCK]).astype(BF)
+        r1 = r[BLOCK:] * jnp.exp2(before[BLOCK:] - mid1).astype(BF)
+        k1 = k[BLOCK:] * jnp.exp2(mid1 - cum[BLOCK:]).astype(BF)
+        r1c = r[BLOCK:] * jnp.exp2(before[BLOCK:] - end0).astype(BF)
+        k0c = k[:BLOCK] * jnp.exp2(end0 - cum[:BLOCK]).astype(BF)
+        rin_ref[:BLOCK, c] = r[:BLOCK] * jnp.exp2(before[:BLOCK]).astype(BF)
+        rin_ref[BLOCK:, c] = r[BLOCK:] * jnp.exp2(before[BLOCK:]).astype(BF)
+        bonus = (r.astype(F32) * u_ref[:, c] * k.astype(F32)).astype(BF)
+        own = mm(bonus, head_ones(1.0)) * v.astype(F32)
         for p in range(WIDE // PAIR):
             s = slice(p * PAIR, (p + 1) * PAIR)
             o = slice(at + p * PAIR, at + (p + 1) * PAIR)
@@ -169,27 +179,29 @@
     for g in range(groups):
         logs = msg_ref[g, 4].astype(F32)
         out_ref[g] = state.astype(BF)
-        decay = jnp.exp(logs[0:1] + logs[1:2])
+        decay = jnp.exp2(logs[0:1] + logs[1:2])
         state = state * decay + msg_ref[g, 0:4].reshape(8, PAIR).astype(F32)
 
 
 def finish_kernel(
     c_ref,
-    s_hbm,
-    out_hbm,
-    rin_hbm,
-    sg_hbm,
+    s_ref,
+    early_out,
+    early_rin,
+    early_sg,
+    late_out,
+    late_rin,
+    late_sg,
     w1_hbm,
     w2_hbm,
     y_hbm,
-    s_ref,
     out_buf,
     rin_buf,
     sg_buf,
     w_buf,
+    entering,
     gated,
     y_buf,
-    s_sem,
     in_sems,
     w_sems,
     y_sems,
@@ -199,15 +211,21 @@
     wide = out_buf.shape[1] // chunks
     tile = y_buf.shape[1] // tiles
     half = out_buf.shape[1] // 2
-    loads = [
-        [
-            pltpu.make_async_copy(
-                src.at[:, pl.ds(i * wide, wide)], dst.at[:, pl.ds(i * wide, wide)], in_sems.at[j, i]
-            )
-            for j, (src, dst) in enumerate(((out_hbm, out_buf), (rin_hbm, rin_buf), (sg_hbm, sg_buf)))
-        ]
-        for i in range(chunks)
-    ]
+    split = early_out.shape[1] // wide
+    loads = []
+    for i in range(chunks):
+        if i < split:
+            at, sources = i * wide, (early_out, early_rin, early_sg)
+        else:
+            at, sources = (i - split) * wide, (late_out, late_rin, late_sg)
+        loads.append(
+            [
+                pltpu.make_async_copy(
+                    src.at[:, pl.ds(at, wide)], dst.at[:, pl.ds(i * wide, wide)], in_sems.at[j, i]
+                )
+                for j, (src, dst) in enumerate(zip(sources, (out_buf, rin_buf, sg_buf)))
+            ]
+        )
 
     def cols(t):
         return pl.ds(pl.multiple_of(t * tile, tile), tile)
@@ -219,38 +237,46 @@
     def store(t):
         return pltpu.make_async_copy(y_buf.at[:, cols(t)], y_hbm.at[:, cols(t)], y_sems.at[t])
 
-    entering_load = pltpu.make_async_copy(s_hbm, s_ref, s_sem)
-    entering_load.start()
     for chunk in loads:
         for one in chunk:
             one.start()
-    entering_load.wait()
     first = lax.broadcasted_iota(jnp.int32, (HALF, PAIR), 1) < HALF
     zero = jnp.zeros((HALF, PAIR), BF)
     share = head_ones(1.0 / HALF)
+    parts = out_buf.shape[1] // WIDE
+    per = parts // chunks
+
+    def place(part):
+        to = part * WIDE % half
+        return part * WIDE // half, slice(to, to + WIDE)
+
+    for part in range(parts):
+        for p in range(2):
+            pair = s_ref[2 * part + p]
+            lanes = slice(p * PAIR, (p + 1) * PAIR)
+            rest = slice((1 - p) * PAIR, (2 - p) * PAIR)
+            entering[part, p * PAIR : p * PAIR + HALF, lanes] = jnp.where(first, pair, zero)
+            entering[part, p * PAIR + HALF : (p + 1) * PAIR, lanes] = jnp.where(first, zero, pair)
+            entering[part, p * PAIR : (p + 1) * PAIR, rest] = jnp.zeros((PAIR, PAIR), BF)
     for i in range(chunks):
         for one in loads[i]:
             one.wait()
-        fetch(0, i).start()
-        fetch(1, i).start()
-        for part in range(i * wide // WIDE, (i + 1) * wide // WIDE):
+        for t in WEIGHT_STAGES[i]:
+            fetch(0, t).start()
+            fetch(1, t).start()
+        for part in range(i * per, (i + 1) * per):
             c = slice(part * WIDE, (part + 1) * WIDE)
-            a, b = s_ref[2 * part], s_ref[2 * part + 1]
-            entering = jnp.concatenate(
-                [
-                    jnp.concatenate([jnp.where(first, a, zero), zero], axis=1),
-                    jnp.concatenate([jnp.where(first, zero, a), zero], axis=1),
-                    jnp.concatenate([zero, jnp.where(first, b, zero)], axis=1),
-                    jnp.concatenate([zero, jnp.where(first, zero, b)], axis=1),
-                ],
-                axis=0,
-            )
-            wkv = out_buf[:, c] + mm_nt(rin_buf[:, c], entering)
-            var = mm((wkv * wkv).astype(BF), share)
-            to = part * WIDE % half
-            gated[part * WIDE // half, :, to : to + WIDE] = (
-                wkv * lax.rsqrt(var + EPS) * sg_buf[:, c].astype(F32)
-            ).astype(BF)
+            side, to = place(part)
+            wkv = out_buf[:, c] + mm_nt(rin_buf[:, c], entering[part])
+            out_buf[:, c] = wkv
+            gated[side, :, to] = (wkv * wkv).astype(BF)
+    for part in range(parts):
+        c = slice(part * WIDE, (part + 1) * WIDE)
+        side, to = place(part)
+        var = mm(gated[side, :, to], share)
+        gated[side, :, to] = (
+            out_buf[:, c] * lax.rsqrt(var + EPS) * sg_buf[:, c].astype(F32)
+        ).astype(BF)
 
     mine = c_ref[0]
 
@@ -258,10 +284,10 @@
         fetch(0, t).wait()
         fetch(1, t).wait()
 
-        @pl.when(t + chunks < tiles)
+        @pl.when(t + WEIGHTS_AHEAD < tiles)
         def _():
-            fetch(0, t + chunks).start()
-            fetch(1, t + chunks).start()
+            fetch(0, t + WEIGHTS_AHEAD).start()
+            fetch(1, t + WEIGHTS_AHEAD).start()
 
         y = mm(gated[mine], w_buf[0, :, cols(t)]) + mm(gated[1 - mine], w_buf[1, :, cols(t)])
         y_buf[:, cols(t)] = y.astype(BF)
@@ -277,8 +303,12 @@
     return pltpu.CompilerParams(dimension_semantics=semantics, vmem_limit_bytes=limit)
 
 
+def in_hbm(x):
+    return pltpu.with_memory_space_constraint(x, pltpu.HBM)
+
+
 def call_state(k, v, w, groups):
-    chunks = 4
+    chunks = 2
     any_block = pl.BlockSpec(memory_space=pl.ANY)
     shape = (groups, 5, 2, PAIR)
     return pl.pallas_call(
@@ -311,13 +341,13 @@
         out_specs=[out_blk] * 3,
         out_shape=[jax.ShapeDtypeStruct((tokens, count * wide), t) for t in (F32, BF, BF)],
         compiler_params=params("arbitrary"),
-        cost_estimate=pl.CostEstimate(flops=4 << 30, bytes_accessed=10 << 20, transcendentals=4 << 20),
+        cost_estimate=pl.CostEstimate(flops=count << 32, bytes_accessed=count << 21, transcendentals=count << 20),
         name="local",
     )(r, k, v, w, g, bonus, gain)
 
 
 def call_scan(msg, anchor):
-    anchor = pltpu.with_memory_space_constraint(anchor, pltpu.HBM)
+    anchor = in_hbm(anchor)
     return pl.pallas_call(
         scan_kernel,
         in_specs=[pl.BlockSpec(memory_space=pltpu.VMEM), pl.BlockSpec(memory_space=pl.ANY)],
@@ -327,8 +357,10 @@
     )(msg, anchor)
 
 
-def call_finish(core, out, rin, entering, sg, weight, other_weight):
-    tokens, width = out.shape
+def call_finish(core, entering, early, late, weight, other_weight):
+    tokens, width = early[0].shape[0], 2 * weight.shape[0]
+    early, late = ([in_hbm(x) for x in part] for part in (early, late))
+    weight, other_weight = in_hbm(weight), in_hbm(other_weight)
     cols = weight.shape[1]
     chunks, tiles = 4, 8
     any_block = pl.BlockSpec(memory_space=pl.ANY)
@@ -336,47 +368,51 @@
         finish_kernel,
         in_specs=[
             pl.BlockSpec(memory_space=pltpu.SMEM),
+            pl.BlockSpec(memory_space=pltpu.VMEM),
         ]
-        + [any_block] * 6,
+        + [any_block] * 8,
         out_specs=any_block,
         out_shape=jax.ShapeDtypeStruct((tokens, cols), BF),
         scratch_shapes=[
-            pltpu.VMEM(entering.shape, BF),
-            pltpu.VMEM(out.shape, F32),
-            pltpu.VMEM(out.shape, BF),
-            pltpu.VMEM(out.shape, BF),
+            pltpu.VMEM((tokens, width), F32),
+            pltpu.VMEM((tokens, width), BF),
+            pltpu.VMEM((tokens, width), BF),
             pltpu.VMEM((2, width // 2, cols), BF),
+            pltpu.VMEM((width // WIDE, WIDE, WIDE), BF),
             pltpu.VMEM((2, tokens, width // 2), BF),
             pltpu.VMEM((tokens, cols), BF),
-            pltpu.SemaphoreType.DMA,
             pltpu.SemaphoreType.DMA((3, chunks)),
             pltpu.SemaphoreType.DMA((2, tiles)),
             pltpu.SemaphoreType.DMA((tiles,)),
         ],
-        compiler_params=params(limit=58 << 20),
+        compiler_params=params(limit=32 << 20),
         name="finish",
-    )(core.reshape(1).astype(jnp.int32), entering, out, rin, sg, weight, other_weight)
+    )(core.reshape(1).astype(jnp.int32), entering, *early, *late, weight, other_weight)
 
 
 def shards(r, k, v, w, g, bonus, gain, weight):
     groups = lax.axis_size(SEQ_HEAD)
     core = lax.axis_index("head")
-    r, k, v, w, g = (pltpu.with_memory_space_constraint(x, pltpu.HBM) for x in (r, k, v, w, g))
+    r, k, v, w, g = (in_hbm(x) for x in (r, k, v, w, g))
     swap = [(0, 1), (1, 0)]
     other_weight = lax.ppermute(weight, "head", swap)
+    msg = call_state(k, v, w, groups)
+    msg, bonus, gain = lax.optimization_barrier((msg, bonus, gain))
+    msg = lax.all_to_all(msg, SEQ_HEAD, split_axis=0, concat_axis=0, tiled=True)
     small = jnp.stack([bonus.reshape(-1), gain])
     other_small = lax.ppermute(small, "head", swap)
     low = jnp.where(core == 0, small, other_small)
     high = jnp.where(core == 0, other_small, small)
     small = jnp.concatenate([low, high], axis=1)
     bonus, gain = small[0:1], small[1:2]
-    msg = call_state(k, v, w, groups)
-    msg = lax.all_to_all(msg, SEQ_HEAD, split_axis=0, concat_axis=0, tiled=True)
-    out, rin, sg = call_local(r, k, v, w, g, bonus, gain, 0, r.shape[1] // (2 * WIDE))
-    entering = call_scan(msg, rin)
+    steps = r.shape[1] // (2 * WIDE)
+    first = 2
+    early = call_local(r, k, v, w, g, bonus, gain, 0, first)
+    entering = call_scan(msg, early[1])
     entering = lax.all_to_all(entering, SEQ_HEAD, split_axis=0, concat_axis=0, tiled=True)
+    late = call_local(r, k, v, w, g, bonus, gain, first, steps - first)
     entering = entering.reshape(-1, HALF, PAIR)
-    return call_finish(core, out, rin, entering, sg, weight, other_weight)
+    return call_finish(core, entering, early, late, weight, other_weight)
 
 
 def solution(mesh):

time: 60.9 us -> 53.9 us (0.89)
  blocking collectives: 18.7 us -> 0 us
  waiting for transfers between devices: 2.1 us -> 11.2 us
  starting transfers between devices: 12.1 us -> 16.5 us
  other arithmetic: 1.33 us -> 0.64 us
  local copies, waits for them, and re-layouts: 0.78 us -> 0.09 us
    all_to_all x1 -> x0, blocking collectives: 18.7 us -> none  [shards(): lax.all_to_all(entering, SEQ_HEAD, split_axis=0, concat_axis=0, tiled=True)]
    all_to_all x0 -> x1, waiting for transfers between devices: none -> 5.56 us  [shards(): lax.all_to_all(entering, SEQ_HEAD, split_axis=0, concat_axis=0, tiled=True)]
    all_to_all x0 -> x1, starting transfers between devices: none -> 4.4 us  [shards(): lax.all_to_all(entering, SEQ_HEAD, split_axis=0, concat_axis=0, tiled=True)]
    all_to_all x1, waiting for transfers between devices: 2.1 us -> 5.6 us  [shards(): msg = lax.all_to_all(msg, SEQ_HEAD, split_axis=0, concat_axis=0, tiled=True)]
    pallas_call x1 -> x2, Pallas kernels: 9.01 us -> 11 us  [call_local(): pl.pallas_call(local_kernel, grid=(count,), in_specs=[blk] * 5 + [row] *...]
    pallas_call x1, Pallas kernels: 5.38 us -> 3.41 us  [call_state(): pl.pallas_call(state_kernel, in_specs=[any_block] * 3, out_specs=any_bloc...]
    pallas_call x1, Pallas kernels: 10.9 us -> 9.81 us  [call_finish(): pl.pallas_call(finish_kernel, in_specs=[pl.BlockSpec(memory_space=pltpu.S...]
    another operation x1, local copies, waits for them, and re-layouts: 0.77 us -> 0.08 us  [shards(): small = jnp.stack([bonus.reshape(-1), gain])]
  transfers between devices with their start and end apart: 3 -> 4, of which waited for: 1 -> 2; matrix products, arithmetic and copies ran while one was open for 3% -> 1% of each run, Pallas kernels for 24% -> 29%
where the time goes in v2:
time: 53.9 us; the launch traced here: 53.7 us
  Pallas kernels  25.2 us (47%)
  starting transfers between devices  16.5 us (31%)
  waiting for transfers between devices  11.2 us (21%)
  other arithmetic  0.64 us (1%)
    pallas_call x2, Pallas kernels, call_local(): pl.pallas_call(local_kernel, grid=(count,), in_specs=[blk] * 5 + [row] *...  11 us
    all_to_all x1, starting transfers between devices, shards(): msg = lax.all_to_all(msg, SEQ_HEAD, split_axis=0, concat_axis=0, tiled=True)  10.6 us
    pallas_call x1, Pallas kernels, call_finish(): pl.pallas_call(finish_kernel, in_specs=[pl.BlockSpec(memory_space=pltpu.S...  9.81 us
    all_to_all x1, waiting for transfers between devices, shards(): msg = lax.all_to_all(msg, SEQ_HEAD, split_axis=0, concat_axis=0, tiled=True)  5.6 us
    all_to_all x1, waiting for transfers between devices, shards(): lax.all_to_all(entering, SEQ_HEAD, split_axis=0, concat_axis=0, tiled=True)  5.56 us
    all_to_all x1, starting transfers between devices, shards(): lax.all_to_all(entering, SEQ_HEAD, split_axis=0, concat_axis=0, tiled=True)  4.4 us
    pallas_call x1, Pallas kernels, call_state(): pl.pallas_call(state_kernel, in_specs=[any_block] * 3, out_specs=any_bloc...  3.41 us
    ppermute x1, starting transfers between devices, shards(): other_weight = lax.ppermute(weight, 'head', swap)  1.38 us
  transfers between devices with their start and end apart: 4, of which 2 were waited for; matrix products, arithmetic and copies ran while one was open for 1% of the time, Pallas kernels for 29%

profile of v2, /device:TPU:1, one launch (start us, length us, event | category | flops | bytes accessed | tf_op | source)
XLA Modules:
  0.0 53.7 jit_solution(9653173253589599725)
XLA Ops:
  0.0 0.0 copy-start
  0.0 0.0 copy-start.1
  0.0 1.4 %collective-permute-start.1 = (bf16[1024,4096]{1,0:T(8,128)(2,1)}, bf16[1024,4096]{1,0:T(8,128)(2,1)}, u32[]{:S(2)}, u32[]{:S(2)}) collective-permute-start(bf16[1024,4096]{1,0:T(8,128)(2,1)} %w1_hbm.1), channel_id=1, source_target_pairs={{0,1},{1,0},{2,3},{3,2},{4,5},{5,4},{6,7},{7,6},{8,9},{9,8},{10,11... | collective-permute-start | bytes 25165832 | tf_op jit(solution)/shard_map/ppermute | solution.py:398
  1.4 3.4 %state.1 = bf16[128,5,2,128]{3,2,1,0:T(2,128)(2,1)} custom-call(bf16[256,2048]{1,0:T(8,128)(2,1)} %k_ref.3, bf16[256,2048]{1,0:T(8,128)(2,1)} %v_ref.3, bf16[256,2048]{1,0:T(8,128)(2,1)} %w_ref.3), custom_call_target="tpu_custom_call" | custom-call | flops 4294967296 | bytes 4194304 | tf_op jit(solution)/shard_map/state/pallas_call | solution.py:314
  4.8 0.0 copy-done.1
  4.8 0.1 stack_reshape.3
  4.9 0.0 copy-done
  4.9 0.1 collective-permute-start
  5.0 10.6 %all-to-all-start = ((bf16[128,5,2,128]{3,2,1,0:T(2,128)(2,1)}), bf16[128,5,2,128]{3,2,1,0:T(2,128)(2,1)S(1)}, u32[]{:S(2)}, u32[]{:S(2)}) async-start(bf16[128,5,2,128]{3,2,1,0:T(2,128)(2,1)} %state.1), calls=%async_computation | async-start | bytes 655360 | tf_op jit(solution)/shard_map/all_to_all | solution.py:401
  15.6 0.0 collective-permute-done
  15.7 0.6 %pad_maximum_fusion = (f32[1,2048]{1,0:T(1,128)}, f32[1,2048]{1,0:T(1,128)}) fusion(f32[2,1024]{1,0:T(2,128)S(1)} %get-tuple-element.25, f32[2,1024]{1,0:T(2,128)S(1)} %get-tuple-element.26), kind=kLoop, calls=%fused_computation.3 | loop fusion | flops 4096 | bytes 32768 | tf_op jit(solution)/shard_map/concatenate | solution.py:406
  16.3 5.5 %local.2 = (f32[256,1024]{1,0:T(8,128)}, bf16[256,1024]{1,0:T(8,128)(2,1)}, bf16[256,1024]{1,0:T(8,128)(2,1)}) custom-call(bf16[256,2048]{1,0:T(8,128)(2,1)} %r_ref.3, bf16[256,2048]{1,0:T(8,128)(2,1)} %k_ref.3, bf16[256,2048]{1,0:T(8,128)(2,1)} %v_ref.3, bf16[256,2048]{1,0:T(8,128)(2,1)} %w_ref.3, bf16[256,2048]{1,0:T(8,128)(2,1)} %g_ref.3, ...), custom_call_target="tpu_custom_call" | custom-call | flops 8589934592 | bytes 4194304 | tf_op jit(solution)/shard_map/local/pallas_call | solution.py:337
  21.8 5.6 %all-to-all-done.msg_ref = bf16[128,5,2,128]{3,2,1,0:T(2,128)(2,1)S(1)} async-done(((bf16[128,5,2,128]{3,2,1,0:T(2,128)(2,1)}), bf16[128,5,2,128]{3,2,1,0:T(2,128)(2,1)S(1)}, u32[]{:S(2)}, u32[]{:S(2)}) %all-to-all-start) | async-done | bytes 327712 | tf_op jit(solution)/shard_map/all_to_all | solution.py:401
  27.4 1.0 %scan.1 = bf16[128,8,128]{2,1,0:T(8,128)(2,1)} custom-call(bf16[128,5,2,128]{3,2,1,0:T(2,128)(2,1)S(1)} %all-to-all-done.msg_ref, bf16[256,1024]{1,0:T(8,128)(2,1)} %get-tuple-element.17.after_ref.early_rin), custom_call_target="tpu_custom_call" | custom-call | tf_op jit(solution)/shard_map/scan/pallas_call | solution.py:351
  28.4 4.4 %all-to-all-start.1 = ((bf16[128,8,128]{2,1,0:T(8,128)(2,1)}), bf16[128,8,128]{2,1,0:T(8,128)(2,1)S(1)}, u32[]{:S(2)}, u32[]{:S(2)}) async-start(bf16[128,8,128]{2,1,0:T(8,128)(2,1)} %scan.1), calls=%async_computation.1 | async-start | bytes 524288 | tf_op jit(solution)/shard_map/all_to_all | solution.py:412
  32.8 5.5 %local.3 = (f32[256,1024]{1,0:T(8,128)}, bf16[256,1024]{1,0:T(8,128)(2,1)}, bf16[256,1024]{1,0:T(8,128)(2,1)}) custom-call(bf16[256,2048]{1,0:T(8,128)(2,1)} %r_ref.3, bf16[256,2048]{1,0:T(8,128)(2,1)} %k_ref.3, bf16[256,2048]{1,0:T(8,128)(2,1)} %v_ref.3, bf16[256,2048]{1,0:T(8,128)(2,1)} %w_ref.3, bf16[256,2048]{1,0:T(8,128)(2,1)} %g_ref.3, ...), custom_call_target="tpu_custom_call" | custom-call | flops 8589934592 | bytes 4194304 | tf_op jit(solution)/shard_map/local/pallas_call | solution.py:337
  38.3 5.6 %all-to-all-done.1 = bf16[128,8,128]{2,1,0:T(8,128)(2,1)S(1)} async-done(((bf16[128,8,128]{2,1,0:T(8,128)(2,1)}), bf16[128,8,128]{2,1,0:T(8,128)(2,1)S(1)}, u32[]{:S(2)}, u32[]{:S(2)}) %all-to-all-start.1) | async-done | bytes 262176 | tf_op jit(solution)/shard_map/all_to_all | solution.py:412
  43.9 0.0 collective-permute-done.1.w2_hbm
  43.9 9.8 %finish.1 = bf16[256,4096]{1,0:T(8,128)(2,1)} custom-call(s32[1]{0:T(128)} %bitcast.c_ref, bf16[16,64,128]{2,1,0:T(8,128)(2,1)S(1)} %bitcast.3, f32[256,1024]{1,0:T(8,128)} %get-tuple-element.18.early_out, bf16[256,1024]{1,0:T(8,128)(2,1)} %get-tuple-element.17.after_ref.early_rin, bf16[256,1024]{1,0:T(8,128)(2,1)} %get-tuple-element.19.early_sg, ...), custom_call_target="tpu_custom_call" | custom-call | tf_op jit(solution)/shard_map/finish/pallas_call | solution.py:367
  (2 shorter events, 0.0 us)
Async XLA Ops:
  0.0 4.9 %copy-start = (f32[1024]{0:T(1024)S(1)}, f32[1024]{0:T(1024)}, u32[]{:S(2)}) copy-start(f32[1024]{0:T(1024)} %param.14) | copy-start | bytes 12292
  0.0 4.8 %copy-start.1 = (f32[16,64]{1,0:T(8,128)S(1)}, f32[16,64]{1,0:T(8,128)}, u32[]{:S(2)}) copy-start(f32[16,64]{1,0:T(8,128)} %param.13) | copy-start | bytes 12292
  0.0 43.9 %collective-permute-start.1 = (bf16[1024,4096]{1,0:T(8,128)(2,1)}, bf16[1024,4096]{1,0:T(8,128)(2,1)}, u32[]{:S(2)}, u32[]{:S(2)}) collective-permute-start(bf16[1024,4096]{1,0:T(8,128)(2,1)} %w1_hbm.1), channel_id=1, source_target_pairs={{0,1},{1,0},{2,3},{3,2},{4,5},{5,4},{6,7},{7,6},{8,9},{9,8},{10,11... | collective-permute-start | bytes 25165832 | tf_op jit(solution)/shard_map/ppermute | solution.py:398
  4.9 10.7 %collective-permute-start = (f32[2,1024]{1,0:T(2,128)S(1)}, f32[2,1024]{1,0:T(2,128)S(1)}, u32[]{:S(2)}, u32[]{:S(2)}) collective-permute-start(f32[2,1024]{1,0:T(2,128)S(1)} %pad_maximum_fusion.1), channel_id=1, source_target_pairs={{0,1},{1,0},{2,3},{3,2},{4,5},{5,4},{6,7},{7,6},{8,9},{9,8},{10,11... | collective-permute-start | bytes 24584 | tf_op jit(solution)/shard_map/ppermute | solution.py:403
  5.0 22.4 %all-to-all-start = ((bf16[128,5,2,128]{3,2,1,0:T(2,128)(2,1)}), bf16[128,5,2,128]{3,2,1,0:T(2,128)(2,1)S(1)}, u32[]{:S(2)}, u32[]{:S(2)}) async-start(bf16[128,5,2,128]{3,2,1,0:T(2,128)(2,1)} %state.1), calls=%async_computation | async-start | bytes 655360 | tf_op jit(solution)/shard_map/all_to_all | solution.py:401
  28.4 15.5 %all-to-all-start.1 = ((bf16[128,8,128]{2,1,0:T(8,128)(2,1)}), bf16[128,8,128]{2,1,0:T(8,128)(2,1)S(1)}, u32[]{:S(2)}, u32[]{:S(2)}) async-start(bf16[128,8,128]{2,1,0:T(8,128)(2,1)} %scan.1), calls=%async_computation.1 | async-start | bytes 524288 | tf_op jit(solution)/shard_map/all_to_all | solution.py:412

commit v3 on v2

--- a/solution.py
+++ b/solution.py
@@ -1,5 +1,3 @@
-import functools
-
 import jax
 import jax.numpy as jnp
 from jax import lax
@@ -7,6 +5,7 @@
 from jax.experimental.pallas import tpu as pltpu
 from jax.sharding import Mesh
 from jax.sharding import PartitionSpec as P
+
 
 BLOCK = 128
 HALF = 64
@@ -16,8 +15,8 @@
 EPS = 1e-05
 LOG2E = 1.4426950408889634
 LOG2LOG2E = 0.5287663729448977
-WEIGHT_STAGES = ((0, 1), (2, 3), (4,), (5,))
-WEIGHTS_AHEAD = 6
+WEIGHT_STAGES = ((0, 1, 2), (3, 4), (5, 6), (7,))
+TILES_AHEAD = 8
 BF = jnp.bfloat16
 F32 = jnp.float32
 
@@ -119,9 +118,54 @@
 
 
 def local_kernel(
-    r_ref, k_ref, v_ref, w_ref, g_ref, u_ref, gain_ref, out_ref, rin_ref, sg_ref
+    h_ref,
+    u_ref,
+    gain_ref,
+    r_hbm,
+    k_hbm,
+    v_hbm,
+    w_hbm,
+    g_hbm,
+    out_hbm,
+    rin_hbm,
+    sg_hbm,
+    r_ref,
+    k_ref,
+    v_ref,
+    w_ref,
+    g_ref,
+    out_ref,
+    rin_ref,
+    sg_ref,
+    in_sems,
+    out_sems,
 ):
-    tokens = r_ref.shape[0]
+    tokens, half = r_ref.shape
+    chunks = in_sems.shape[1]
+    wide = half // chunks
+    sources = (w_hbm, g_hbm, r_hbm, k_hbm, v_hbm)
+    buffers = (w_ref, g_ref, r_ref, k_ref, v_ref)
+    results = (out_ref, rin_ref, sg_ref)
+    targets = (out_hbm, rin_hbm, sg_hbm)
+
+    def load(i):
+        at = pl.ds(pl.multiple_of(h_ref[0] * half + i * wide, wide), wide)
+        to = pl.ds(i * wide, wide)
+        return [
+            pltpu.make_async_copy(src.at[:, at], dst.at[:, to], in_sems.at[j, i])
+            for j, (src, dst) in enumerate(zip(sources, buffers))
+        ]
+
+    def store(i):
+        at = pl.ds(i * wide, wide)
+        return [
+            pltpu.make_async_copy(src.at[:, at], dst.at[:, at], out_sems.at[j, i])
+            for j, (src, dst) in enumerate(zip(results, targets))
+        ]
+
+    for i in range(chunks):
+        for one in load(i):
+            one.start()
     row, col = grid2(tokens, tokens)
     upto = jnp.where(col <= row, -1.0, 0.0).astype(BF)
     prior = jnp.where(col < row, -1.0, 0.0).astype(BF)
@@ -140,7 +184,7 @@
             a, b = jnp.where(strict, a, 0.0), jnp.where(strict, b, 0.0)
         return jnp.concatenate([a, b], axis=1).astype(BF)
 
-    for part in range(r_ref.shape[1] // WIDE):
+    def compute(part):
         at = part * WIDE
         c = slice(at, at + WIDE)
         gate = g_ref[:, c].astype(F32)
@@ -160,7 +204,9 @@
         k0c = k[:BLOCK] * jnp.exp2(end0 - cum[:BLOCK]).astype(BF)
         rin_ref[:BLOCK, c] = r[:BLOCK] * jnp.exp2(before[:BLOCK]).astype(BF)
         rin_ref[BLOCK:, c] = r[BLOCK:] * jnp.exp2(before[BLOCK:]).astype(BF)
-        bonus = (r.astype(F32) * u_ref[:, c] * k.astype(F32)).astype(BF)
+        heads = range(at // HALF, (at + WIDE) // HALF)
+        u = jnp.concatenate([u_ref[h : h + 1] for h in heads], axis=1)
+        bonus = (r.astype(F32) * u * k.astype(F32)).astype(BF)
         own = mm(bonus, head_ones(1.0)) * v.astype(F32)
         for p in range(WIDE // PAIR):
             s = slice(p * PAIR, (p + 1) * PAIR)
@@ -169,8 +215,19 @@
             s10 = side(mm_nt(stacked(r1c[:, s]), k0c[:, s]), False)
             s11 = side(mm_nt(stacked(r1[:, s]), k1[:, s]), True)
             v0, v1 = stacked(v[:BLOCK, s]), stacked(v[BLOCK:, s])
-            out_ref[:BLOCK, o] = mm(s00, v0) + own[:BLOCK, s]
-            out_ref[BLOCK:, o] = mm(s10, v0) + mm(s11, v1) + own[BLOCK:, s]
+            out_ref[:BLOCK, o] = (mm(s00, v0) + own[:BLOCK, s]).astype(BF)
+            out_ref[BLOCK:, o] = (mm(s10, v0) + mm(s11, v1) + own[BLOCK:, s]).astype(BF)
+
+    for i in range(chunks):
+        for one in load(i):
+            one.wait()
+        for part in range(i * wide // WIDE, (i + 1) * wide // WIDE):
+            compute(part)
+        for one in store(i):
+            one.start()
+    for i in range(chunks):
+        for one in store(i):
+            one.wait()
 
 
 def scan_kernel(msg_ref, after_ref, out_ref):
@@ -186,12 +243,12 @@
 def finish_kernel(
     c_ref,
     s_ref,
-    early_out,
-    early_rin,
-    early_sg,
-    late_out,
-    late_rin,
-    late_sg,
+    mine_out,
+    mine_rin,
+    mine_sg,
+    other_out,
+    other_rin,
+    other_sg,
     w1_hbm,
     w2_hbm,
     y_hbm,
@@ -199,6 +256,7 @@
     rin_buf,
     sg_buf,
     w_buf,
+    wkv_buf,
     entering,
     gated,
     y_buf,
@@ -206,26 +264,22 @@
     w_sems,
     y_sems,
 ):
-    chunks = in_sems.shape[1]
+    chunks = in_sems.shape[2]
     tiles = y_sems.shape[0]
-    wide = out_buf.shape[1] // chunks
+    half = out_buf.shape[2]
+    wide = half // chunks
     tile = y_buf.shape[1] // tiles
-    half = out_buf.shape[1] // 2
-    split = early_out.shape[1] // wide
-    loads = []
-    for i in range(chunks):
-        if i < split:
-            at, sources = i * wide, (early_out, early_rin, early_sg)
-        else:
-            at, sources = (i - split) * wide, (late_out, late_rin, late_sg)
-        loads.append(
-            [
-                pltpu.make_async_copy(
-                    src.at[:, pl.ds(at, wide)], dst.at[:, pl.ds(i * wide, wide)], in_sems.at[j, i]
-                )
-                for j, (src, dst) in enumerate(zip(sources, (out_buf, rin_buf, sg_buf)))
-            ]
-        )
+    parts = half // WIDE
+    per = parts // chunks
+    sources = ((mine_out, mine_rin, mine_sg), (other_out, other_rin, other_sg))
+    buffers = (out_buf, rin_buf, sg_buf)
+
+    def load(side, i):
+        at = pl.ds(i * wide, wide)
+        return [
+            pltpu.make_async_copy(src.at[:, at], dst.at[side, :, at], in_sems.at[j, side, i])
+            for j, (src, dst) in enumerate(zip(sources[side], buffers))
+        ]
 
     def cols(t):
         return pl.ds(pl.multiple_of(t * tile, tile), tile)
@@ -237,59 +291,55 @@
     def store(t):
         return pltpu.make_async_copy(y_buf.at[:, cols(t)], y_hbm.at[:, cols(t)], y_sems.at[t])
 
-    for chunk in loads:
-        for one in chunk:
-            one.start()
+    for side in range(2):
+        for i in range(chunks):
+            for one in load(side, i):
+                one.start()
     first = lax.broadcasted_iota(jnp.int32, (HALF, PAIR), 1) < HALF
     zero = jnp.zeros((HALF, PAIR), BF)
     share = head_ones(1.0 / HALF)
-    parts = out_buf.shape[1] // WIDE
-    per = parts // chunks
-
-    def place(part):
-        to = part * WIDE % half
-        return part * WIDE // half, slice(to, to + WIDE)
-
-    for part in range(parts):
-        for p in range(2):
-            pair = s_ref[2 * part + p]
-            lanes = slice(p * PAIR, (p + 1) * PAIR)
-            rest = slice((1 - p) * PAIR, (2 - p) * PAIR)
-            entering[part, p * PAIR : p * PAIR + HALF, lanes] = jnp.where(first, pair, zero)
-            entering[part, p * PAIR + HALF : (p + 1) * PAIR, lanes] = jnp.where(first, zero, pair)
-            entering[part, p * PAIR : (p + 1) * PAIR, rest] = jnp.zeros((PAIR, PAIR), BF)
-    for i in range(chunks):
-        for one in loads[i]:
-            one.wait()
-        for t in WEIGHT_STAGES[i]:
-            fetch(0, t).start()
-            fetch(1, t).start()
-        for part in range(i * per, (i + 1) * per):
+    for side in range(2):
+        base = (c_ref[0] if side == 0 else 1 - c_ref[0]) * (half // PAIR)
+        for part in range(parts):
+            for p in range(2):
+                pair = s_ref[base + 2 * part + p]
+                lanes = slice(p * PAIR, (p + 1) * PAIR)
+                rest = slice((1 - p) * PAIR, (2 - p) * PAIR)
+                low, high = p * PAIR, p * PAIR + HALF
+                entering[side, part, low:high, lanes] = jnp.where(first, pair, zero)
+                entering[side, part, high : low + PAIR, lanes] = jnp.where(first, zero, pair)
+                entering[side, part, low : low + PAIR, rest] = jnp.zeros((PAIR, PAIR), BF)
+    for side in range(2):
+        for i in range(chunks):
+            for one in load(side, i):
+                one.wait()
+            for t in WEIGHT_STAGES[side * chunks + i]:
+                fetch(0, t).start()
+                fetch(1, t).start()
+            for part in range(i * per, (i + 1) * per):
+                c = slice(part * WIDE, (part + 1) * WIDE)
+                across = mm_nt(rin_buf[side, :, c], entering[side, part])
+                wkv = out_buf[side, :, c].astype(F32) + across
+                wkv_buf[side, :, c] = wkv
+                gated[side, :, c] = (wkv * wkv).astype(BF)
+    for side in range(2):
+        for part in range(parts):
             c = slice(part * WIDE, (part + 1) * WIDE)
-            side, to = place(part)
-            wkv = out_buf[:, c] + mm_nt(rin_buf[:, c], entering[part])
-            out_buf[:, c] = wkv
-            gated[side, :, to] = (wkv * wkv).astype(BF)
-    for part in range(parts):
-        c = slice(part * WIDE, (part + 1) * WIDE)
-        side, to = place(part)
-        var = mm(gated[side, :, to], share)
-        gated[side, :, to] = (
-            out_buf[:, c] * lax.rsqrt(var + EPS) * sg_buf[:, c].astype(F32)
-        ).astype(BF)
-
-    mine = c_ref[0]
+            var = mm(gated[side, :, c], share)
+            gated[side, :, c] = (
+                wkv_buf[side, :, c] * lax.rsqrt(var + EPS) * sg_buf[side, :, c].astype(F32)
+            ).astype(BF)
 
     def project(t, carry):
         fetch(0, t).wait()
         fetch(1, t).wait()
 
-        @pl.when(t + WEIGHTS_AHEAD < tiles)
+        @pl.when(t + TILES_AHEAD < tiles)
         def _():
-            fetch(0, t + WEIGHTS_AHEAD).start()
-            fetch(1, t + WEIGHTS_AHEAD).start()
-
-        y = mm(gated[mine], w_buf[0, :, cols(t)]) + mm(gated[1 - mine], w_buf[1, :, cols(t)])
+            fetch(0, t + TILES_AHEAD).start()
+            fetch(1, t + TILES_AHEAD).start()
+
+        y = mm(gated[0], w_buf[0, :, cols(t)]) + mm(gated[1], w_buf[1, :, cols(t)])
         y_buf[:, cols(t)] = y.astype(BF)
         store(t).start()
         return carry
@@ -299,8 +349,8 @@
         store(t).wait()
 
 
-def params(*semantics, limit=66_000_000):
-    return pltpu.CompilerParams(dimension_semantics=semantics, vmem_limit_bytes=limit)
+def params(limit=66_000_000):
+    return pltpu.CompilerParams(vmem_limit_bytes=limit)
 
 
 def in_hbm(x):
@@ -328,22 +378,23 @@
     )(k, v, w)
 
 
-def call_local(r, k, v, w, g, bonus, gain, start, count):
-    tokens = r.shape[0]
-    wide = 2 * WIDE
-    blk = pl.BlockSpec((tokens, wide), lambda i: (0, i + start))
-    row = pl.BlockSpec((1, wide), lambda i: (0, i + start))
-    out_blk = pl.BlockSpec((tokens, wide), lambda i: (0, i))
+def call_local(side, r, k, v, w, g, bonus, gain):
+    tokens, half = r.shape[0], gain.shape[1]
+    chunks = 2
+    any_block = pl.BlockSpec(memory_space=pl.ANY)
+    vmem_block = pl.BlockSpec(memory_space=pltpu.VMEM)
+    block = (tokens, half)
     return pl.pallas_call(
         local_kernel,
-        grid=(count,),
-        in_specs=[blk] * 5 + [row] * 2,
-        out_specs=[out_blk] * 3,
-        out_shape=[jax.ShapeDtypeStruct((tokens, count * wide), t) for t in (F32, BF, BF)],
-        compiler_params=params("arbitrary"),
-        cost_estimate=pl.CostEstimate(flops=count << 32, bytes_accessed=count << 21, transcendentals=count << 20),
+        in_specs=[pl.BlockSpec(memory_space=pltpu.SMEM)] + [vmem_block] * 2 + [any_block] * 5,
+        out_specs=[any_block] * 3,
+        out_shape=[pltpu.HBM(block, BF)] * 3,
+        scratch_shapes=[pltpu.VMEM(block, BF)] * 8
+        + [pltpu.SemaphoreType.DMA((5, chunks)), pltpu.SemaphoreType.DMA((3, chunks))],
+        compiler_params=params(limit=32 << 20),
+        cost_estimate=pl.CostEstimate(flops=8 << 30, bytes_accessed=4 << 20, transcendentals=2 << 20),
         name="local",
-    )(r, k, v, w, g, bonus, gain)
+    )(side, bonus, gain, r, k, v, w, g)
 
 
 def call_scan(msg, anchor):
@@ -357,62 +408,53 @@
     )(msg, anchor)
 
 
-def call_finish(core, entering, early, late, weight, other_weight):
-    tokens, width = early[0].shape[0], 2 * weight.shape[0]
-    early, late = ([in_hbm(x) for x in part] for part in (early, late))
-    weight, other_weight = in_hbm(weight), in_hbm(other_weight)
-    cols = weight.shape[1]
-    chunks, tiles = 4, 8
+def call_finish(core, entering, mine, other, weight, other_weight):
+    half, cols = weight.shape
+    tokens = mine[0].shape[0]
+    chunks, tiles = 2, 8
+    mine, other = ([in_hbm(x) for x in part] for part in (mine, other))
     any_block = pl.BlockSpec(memory_space=pl.ANY)
     return pl.pallas_call(
         finish_kernel,
-        in_specs=[
-            pl.BlockSpec(memory_space=pltpu.SMEM),
-            pl.BlockSpec(memory_space=pltpu.VMEM),
-        ]
+        in_specs=[pl.BlockSpec(memory_space=pltpu.SMEM), pl.BlockSpec(memory_space=pltpu.VMEM)]
         + [any_block] * 8,
         out_specs=any_block,
         out_shape=jax.ShapeDtypeStruct((tokens, cols), BF),
         scratch_shapes=[
-            pltpu.VMEM((tokens, width), F32),
-            pltpu.VMEM((tokens, width), BF),
-            pltpu.VMEM((tokens, width), BF),
-            pltpu.VMEM((2, width // 2, cols), BF),
-            pltpu.VMEM((width // WIDE, WIDE, WIDE), BF),
-            pltpu.VMEM((2, tokens, width // 2), BF),
+            pltpu.VMEM((2, tokens, half), BF),
+            pltpu.VMEM((2, tokens, half), BF),
+            pltpu.VMEM((2, tokens, half), BF),
+            pltpu.VMEM((2, half, cols), BF),
+            pltpu.VMEM((2, tokens, half), F32),
+            pltpu.VMEM((2, half // WIDE, WIDE, WIDE), BF),
+            pltpu.VMEM((2, tokens, half), BF),
             pltpu.VMEM((tokens, cols), BF),
-            pltpu.SemaphoreType.DMA((3, chunks)),
+            pltpu.SemaphoreType.DMA((3, 2, chunks)),
             pltpu.SemaphoreType.DMA((2, tiles)),
             pltpu.SemaphoreType.DMA((tiles,)),
         ],
         compiler_params=params(limit=32 << 20),
         name="finish",
-    )(core.reshape(1).astype(jnp.int32), entering, *early, *late, weight, other_weight)
+    )(core, entering, *mine, *other, in_hbm(weight), in_hbm(other_weight))
 
 
 def shards(r, k, v, w, g, bonus, gain, weight):
     groups = lax.axis_size(SEQ_HEAD)
-    core = lax.axis_index("head")
+    core = lax.axis_index("head").reshape(1).astype(jnp.int32)
     r, k, v, w, g = (in_hbm(x) for x in (r, k, v, w, g))
+    gain = gain.reshape(1, -1)
     swap = [(0, 1), (1, 0)]
     other_weight = lax.ppermute(weight, "head", swap)
     msg = call_state(k, v, w, groups)
-    msg, bonus, gain = lax.optimization_barrier((msg, bonus, gain))
     msg = lax.all_to_all(msg, SEQ_HEAD, split_axis=0, concat_axis=0, tiled=True)
-    small = jnp.stack([bonus.reshape(-1), gain])
-    other_small = lax.ppermute(small, "head", swap)
-    low = jnp.where(core == 0, small, other_small)
-    high = jnp.where(core == 0, other_small, small)
-    small = jnp.concatenate([low, high], axis=1)
-    bonus, gain = small[0:1], small[1:2]
-    steps = r.shape[1] // (2 * WIDE)
-    first = 2
-    early = call_local(r, k, v, w, g, bonus, gain, 0, first)
-    entering = call_scan(msg, early[1])
+    mine = call_local(core, r, k, v, w, g, bonus, gain)
+    entering = call_scan(msg, mine[1])
     entering = lax.all_to_all(entering, SEQ_HEAD, split_axis=0, concat_axis=0, tiled=True)
-    late = call_local(r, k, v, w, g, bonus, gain, first, steps - first)
+    _, bonus, gain = lax.optimization_barrier((mine[1], bonus, gain))
+    bonus, gain = (lax.ppermute(x, "head", swap) for x in (bonus, gain))
+    other = call_local(1 - core, r, k, v, w, g, bonus, gain)
     entering = entering.reshape(-1, HALF, PAIR)
-    return call_finish(core, entering, early, late, weight, other_weight)
+    return call_finish(core, entering, mine, other, weight, other_weight)
 
 
 def solution(mesh):

time: 53.9 us -> 53.2 us (0.987)
  waiting for transfers between devices: 11.2 us -> 10.3 us
  starting transfers between devices: 16.5 us -> 17.2 us
  other arithmetic: 0.64 us -> 0 us
    ppermute x1 -> x2, starting transfers between devices: 0.1 us -> 1.23 us  [shards(): bonus, gain = (lax.ppermute(x, 'head', swap) for x in (bonus, gain))]
    all_to_all x1, waiting for transfers between devices: 5.6 us -> 4.83 us  [shards(): msg = lax.all_to_all(msg, SEQ_HEAD, split_axis=0, concat_axis=0, tiled=True)]
    concatenate x1 -> x0, other arithmetic: 0.61 us -> none  [shards(): small = jnp.concatenate([low, high], axis=1)]
  transfers between devices with their start and end apart: 4 -> 5, of which waited for: 2 -> 2; matrix products, arithmetic and copies ran while one was open for 1% -> 0% of each run, Pallas kernels for 29% -> 30%
where the time goes in v3:
time: 53.2 us; the launch traced here: 52.9 us
  Pallas kernels  25.3 us (48%)
  starting transfers between devices  17.2 us (32%)
  waiting for transfers between devices  10.3 us (19%)
    pallas_call x2, Pallas kernels, call_local(): pl.pallas_call(local_kernel, in_specs=[pl.BlockSpec(memory_space=pltpu.SM...  11.3 us
    all_to_all x1, starting transfers between devices, shards(): msg = lax.all_to_all(msg, SEQ_HEAD, split_axis=0, concat_axis=0, tiled=True)  10.2 us
    pallas_call x1, Pallas kernels, call_finish(): pl.pallas_call(finish_kernel, in_specs=[pl.BlockSpec(memory_space=pltpu.S...  9.63 us
    all_to_all x1, waiting for transfers between devices, shards(): lax.all_to_all(entering, SEQ_HEAD, split_axis=0, concat_axis=0, tiled=True)  5.41 us
    all_to_all x1, waiting for transfers between devices, shards(): msg = lax.all_to_all(msg, SEQ_HEAD, split_axis=0, concat_axis=0, tiled=True)  4.83 us
    all_to_all x1, starting transfers between devices, shards(): lax.all_to_all(entering, SEQ_HEAD, split_axis=0, concat_axis=0, tiled=True)  4.4 us
    pallas_call x1, Pallas kernels, call_state(): pl.pallas_call(state_kernel, in_specs=[any_block] * 3, out_specs=any_bloc...  3.41 us
    ppermute x1, starting transfers between devices, shards(): other_weight = lax.ppermute(weight, 'head', swap)  1.38 us
  transfers between devices with their start and end apart: 5, of which 2 were waited for; matrix products, arithmetic and copies ran while one was open for 0% of the time, Pallas kernels for 30%

profile of v3, /device:TPU:1, one launch (start us, length us, event | category | flops | bytes accessed | tf_op | source)
XLA Modules:
  0.0 52.9 jit_solution(16776515098323692440)
XLA Ops:
  0.0 0.0 copy-start
  0.0 0.0 copy-start.1
  0.0 1.4 %collective-permute-start.2 = (bf16[1024,4096]{1,0:T(8,128)(2,1)}, bf16[1024,4096]{1,0:T(8,128)(2,1)}, u32[]{:S(2)}, u32[]{:S(2)}) collective-permute-start(bf16[1024,4096]{1,0:T(8,128)(2,1)} %w1_hbm.1), channel_id=1, source_target_pairs={{0,1},{1,0},{2,3},{3,2},{4,5},{5,4},{6,7},{7,6},{8,9},{9,8},{10,11... | collective-permute-start | bytes 25165832 | tf_op jit(solution)/shard_map/ppermute | solution.py:447
  1.4 3.4 %state.1 = bf16[128,5,2,128]{3,2,1,0:T(2,128)(2,1)} custom-call(bf16[256,2048]{1,0:T(8,128)(2,1)} %k_hbm.5, bf16[256,2048]{1,0:T(8,128)(2,1)} %v_hbm.5, bf16[256,2048]{1,0:T(8,128)(2,1)} %w_hbm.5), custom_call_target="tpu_custom_call" | custom-call | flops 4294967296 | bytes 4194304 | tf_op jit(solution)/shard_map/state/pallas_call | solution.py:364
  4.8 10.2 %all-to-all-start = ((bf16[128,5,2,128]{3,2,1,0:T(2,128)(2,1)}), bf16[128,5,2,128]{3,2,1,0:T(2,128)(2,1)S(1)}, u32[]{:S(2)}, u32[]{:S(2)}) async-start(bf16[128,5,2,128]{3,2,1,0:T(2,128)(2,1)} %state.1), calls=%async_computation | async-start | bytes 655360 | tf_op jit(solution)/shard_map/all_to_all | solution.py:449
  15.0 0.0 copy-done
  15.0 0.0 copy-done.1
  15.1 5.7 %local.2 = (bf16[256,1024]{1,0:T(8,128)(2,1)}, bf16[256,1024]{1,0:T(8,128)(2,1)}, bf16[256,1024]{1,0:T(8,128)(2,1)}) custom-call(s32[1]{0:T(128)} %bitcast.h_ref.c_ref, f32[16,64]{1,0:T(8,128)S(1)} %copy-done, f32[1,1024]{1,0:T(1,128)S(1)} %bitcast.4, bf16[256,2048]{1,0:T(8,128)(2,1)} %r_hbm.3, bf16[256,2048]{1,0:T(8,128)(2,1)} %k_hbm.5, ...), custom_call_target="tpu_custom_call" | custom-call | flops 8589934592 | bytes 4194304 | tf_op jit(solution)/shard_map/local/pallas_call | solution.py:387
  20.7 1.1 %collective-permute-start.1 = (f32[1,1024]{1,0:T(1,128)S(1)}, f32[1,1024]{1,0:T(1,128)S(1)}, u32[]{:S(2)}, u32[]{:S(2)}) collective-permute-start(f32[1,1024]{1,0:T(1,128)S(1)} %bitcast.5), channel_id=1, source_target_pairs={{0,1},{1,0},{2,3},{3,2},{4,5},{5,4},{6,7},{7,6},{8,9},{9,8},{10,11... | collective-permute-start | bytes 12296 | tf_op jit(solution)/shard_map/ppermute | solution.py:454
  21.9 0.1 collective-permute-start
  22.0 4.8 %all-to-all-done.msg_ref = bf16[128,5,2,128]{3,2,1,0:T(2,128)(2,1)S(1)} async-done(((bf16[128,5,2,128]{3,2,1,0:T(2,128)(2,1)}), bf16[128,5,2,128]{3,2,1,0:T(2,128)(2,1)S(1)}, u32[]{:S(2)}, u32[]{:S(2)}) %all-to-all-start) | async-done | bytes 327712 | tf_op jit(solution)/shard_map/all_to_all | solution.py:449
  26.8 1.0 %scan.1 = bf16[128,8,128]{2,1,0:T(8,128)(2,1)} custom-call(bf16[128,5,2,128]{3,2,1,0:T(2,128)(2,1)S(1)} %all-to-all-done.msg_ref, bf16[256,1024]{1,0:T(8,128)(2,1)} %get-tuple-element.13.after_ref.mine_rin), custom_call_target="tpu_custom_call" | custom-call | tf_op jit(solution)/shard_map/scan/pallas_call | solution.py:402
  27.8 4.4 %all-to-all-start.1 = ((bf16[128,8,128]{2,1,0:T(8,128)(2,1)}), bf16[128,8,128]{2,1,0:T(8,128)(2,1)S(1)}, u32[]{:S(2)}, u32[]{:S(2)}) async-start(bf16[128,8,128]{2,1,0:T(8,128)(2,1)} %scan.1), calls=%async_computation.1 | async-start | bytes 524288 | tf_op jit(solution)/shard_map/all_to_all | solution.py:452
  32.2 0.0 collective-permute-done.1.gain_ref
  32.2 0.0 collective-permute-done.u_ref
  32.2 5.6 %local.3 = (bf16[256,1024]{1,0:T(8,128)(2,1)}, bf16[256,1024]{1,0:T(8,128)(2,1)}, bf16[256,1024]{1,0:T(8,128)(2,1)}) custom-call(s32[1]{0:T(128)S(6)} %sub.3.h_ref, f32[16,64]{1,0:T(8,128)S(1)} %collective-permute-done.u_ref, f32[1,1024]{1,0:T(1,128)S(1)} %collective-permute-done.1.gain_ref, bf16[256,2048]{1,0:T(8,128)(2,1)} %r_hbm.3, ...), custom_call_target="tpu_custom_call" | custom-call | flops 8589934592 | bytes 4194304 | tf_op jit(solution)/shard_map/local/pallas_call | solution.py:387
  37.9 5.4 %all-to-all-done.1 = bf16[128,8,128]{2,1,0:T(8,128)(2,1)S(1)} async-done(((bf16[128,8,128]{2,1,0:T(8,128)(2,1)}), bf16[128,8,128]{2,1,0:T(8,128)(2,1)S(1)}, u32[]{:S(2)}, u32[]{:S(2)}) %all-to-all-start.1) | async-done | bytes 262176 | tf_op jit(solution)/shard_map/all_to_all | solution.py:452
  43.3 0.0 collective-permute-done.2.w2_hbm
  43.3 9.6 %finish.1 = bf16[256,4096]{1,0:T(8,128)(2,1)} custom-call(s32[1]{0:T(128)} %bitcast.h_ref.c_ref, bf16[16,64,128]{2,1,0:T(8,128)(2,1)S(1)} %bitcast.3, bf16[256,1024]{1,0:T(8,128)(2,1)} %get-tuple-element.14.mine_out, bf16[256,1024]{1,0:T(8,128)(2,1)} %get-tuple-element.13.after_ref.mine_rin, bf16[256,1024]{1,0:T(8,128)(2,1)} %get-tuple-element.15.mine_sg, ...), custom_call_target="tpu_custom_call" | custom-call | tf_op jit(solution)/shard_map/finish/pallas_call | solution.py:417
Async XLA Ops:
  0.0 15.0 %copy-start = (f32[16,64]{1,0:T(8,128)S(1)}, f32[16,64]{1,0:T(8,128)}, u32[]{:S(2)}) copy-start(f32[16,64]{1,0:T(8,128)} %u_ref.1) | copy-start | bytes 12292
  0.0 15.0 %copy-start.1 = (f32[1024]{0:T(1024)S(1)}, f32[1024]{0:T(1024)}, u32[]{:S(2)}) copy-start(f32[1024]{0:T(1024)} %param.14) | copy-start | bytes 12292
  0.0 43.3 %collective-permute-start.2 = (bf16[1024,4096]{1,0:T(8,128)(2,1)}, bf16[1024,4096]{1,0:T(8,128)(2,1)}, u32[]{:S(2)}, u32[]{:S(2)}) collective-permute-start(bf16[1024,4096]{1,0:T(8,128)(2,1)} %w1_hbm.1), channel_id=1, source_target_pairs={{0,1},{1,0},{2,3},{3,2},{4,5},{5,4},{6,7},{7,6},{8,9},{9,8},{10,11... | collective-permute-start | bytes 25165832 | tf_op jit(solution)/shard_map/ppermute | solution.py:447
  4.8 22.0 %all-to-all-start = ((bf16[128,5,2,128]{3,2,1,0:T(2,128)(2,1)}), bf16[128,5,2,128]{3,2,1,0:T(2,128)(2,1)S(1)}, u32[]{:S(2)}, u32[]{:S(2)}) async-start(bf16[128,5,2,128]{3,2,1,0:T(2,128)(2,1)} %state.1), calls=%async_computation | async-start | bytes 655360 | tf_op jit(solution)/shard_map/all_to_all | solution.py:449
  20.7 11.5 %collective-permute-start.1 = (f32[1,1024]{1,0:T(1,128)S(1)}, f32[1,1024]{1,0:T(1,128)S(1)}, u32[]{:S(2)}, u32[]{:S(2)}) collective-permute-start(f32[1,1024]{1,0:T(1,128)S(1)} %bitcast.5), channel_id=1, source_target_pairs={{0,1},{1,0},{2,3},{3,2},{4,5},{5,4},{6,7},{7,6},{8,9},{9,8},{10,11... | collective-permute-start | bytes 12296 | tf_op jit(solution)/shard_map/ppermute | solution.py:454
  21.9 10.3 %collective-permute-start = (f32[16,64]{1,0:T(8,128)S(1)}, f32[16,64]{1,0:T(8,128)S(1)}, u32[]{:S(2)}, u32[]{:S(2)}) collective-permute-start(f32[16,64]{1,0:T(8,128)S(1)} %copy-done), channel_id=1, source_target_pairs={{0,1},{1,0},{2,3},{3,2},{4,5},{5,4},{6,7},{7,6},{8,9},{9,8},{10,11... | collective-permute-start | bytes 12296 | tf_op jit(solution)/shard_map/ppermute | solution.py:454
  27.8 15.5 %all-to-all-start.1 = ((bf16[128,8,128]{2,1,0:T(8,128)(2,1)}), bf16[128,8,128]{2,1,0:T(8,128)(2,1)S(1)}, u32[]{:S(2)}, u32[]{:S(2)}) async-start(bf16[128,8,128]{2,1,0:T(8,128)(2,1)} %scan.1), calls=%async_computation.1 | async-start | bytes 524288 | tf_op jit(solution)/shard_map/all_to_all | solution.py:452

commit v4 on v3

--- a/solution.py
+++ b/solution.py
@@ -15,8 +15,7 @@
 EPS = 1e-05
 LOG2E = 1.4426950408889634
 LOG2LOG2E = 0.5287663729448977
-WEIGHT_STAGES = ((0, 1, 2), (3, 4), (5, 6), (7,))
-TILES_AHEAD = 8
+TILES_AHEAD = 4
 BF = jnp.bfloat16
 F32 = jnp.float32
 
@@ -126,27 +125,21 @@
     v_hbm,
     w_hbm,
     g_hbm,
-    out_hbm,
-    rin_hbm,
-    sg_hbm,
+    out_ref,
+    rin_ref,
+    sg_ref,
     r_ref,
     k_ref,
     v_ref,
     w_ref,
     g_ref,
-    out_ref,
-    rin_ref,
-    sg_ref,
     in_sems,
-    out_sems,
 ):
     tokens, half = r_ref.shape
     chunks = in_sems.shape[1]
     wide = half // chunks
     sources = (w_hbm, g_hbm, r_hbm, k_hbm, v_hbm)
     buffers = (w_ref, g_ref, r_ref, k_ref, v_ref)
-    results = (out_ref, rin_ref, sg_ref)
-    targets = (out_hbm, rin_hbm, sg_hbm)
 
     def load(i):
         at = pl.ds(pl.multiple_of(h_ref[0] * half + i * wide, wide), wide)
@@ -154,13 +147,6 @@
         return [
             pltpu.make_async_copy(src.at[:, at], dst.at[:, to], in_sems.at[j, i])
             for j, (src, dst) in enumerate(zip(sources, buffers))
-        ]
-
-    def store(i):
-        at = pl.ds(i * wide, wide)
-        return [
-            pltpu.make_async_copy(src.at[:, at], dst.at[:, at], out_sems.at[j, i])
-            for j, (src, dst) in enumerate(zip(results, targets))
         ]
 
     for i in range(chunks):
@@ -223,11 +209,6 @@
             one.wait()
         for part in range(i * wide // WIDE, (i + 1) * wide // WIDE):
             compute(part)
-        for one in store(i):
-            one.start()
-    for i in range(chunks):
-        for one in store(i):
-            one.wait()
 
 
 def scan_kernel(msg_ref, after_ref, out_ref):
@@ -252,34 +233,19 @@
     w1_hbm,
     w2_hbm,
     y_hbm,
-    out_buf,
-    rin_buf,
-    sg_buf,
     w_buf,
     wkv_buf,
     entering,
     gated,
     y_buf,
-    in_sems,
     w_sems,
     y_sems,
 ):
-    chunks = in_sems.shape[2]
     tiles = y_sems.shape[0]
-    half = out_buf.shape[2]
-    wide = half // chunks
+    half = mine_out.shape[1]
     tile = y_buf.shape[1] // tiles
     parts = half // WIDE
-    per = parts // chunks
-    sources = ((mine_out, mine_rin, mine_sg), (other_out, other_rin, other_sg))
-    buffers = (out_buf, rin_buf, sg_buf)
-
-    def load(side, i):
-        at = pl.ds(i * wide, wide)
-        return [
-            pltpu.make_async_copy(src.at[:, at], dst.at[side, :, at], in_sems.at[j, side, i])
-            for j, (src, dst) in enumerate(zip(sources[side], buffers))
-        ]
+    results = ((mine_out, mine_rin, mine_sg), (other_out, other_rin, other_sg))
 
     def cols(t):
         return pl.ds(pl.multiple_of(t * tile, tile), tile)
@@ -291,10 +257,9 @@
     def store(t):
         return pltpu.make_async_copy(y_buf.at[:, cols(t)], y_hbm.at[:, cols(t)], y_sems.at[t])
 
-    for side in range(2):
-        for i in range(chunks):
-            for one in load(side, i):
-                one.start()
+    for t in range(TILES_AHEAD):
+        fetch(0, t).start()
+        fetch(1, t).start()
     first = lax.broadcasted_iota(jnp.int32, (HALF, PAIR), 1) < HALF
     zero = jnp.zeros((HALF, PAIR), BF)
     share = head_ones(1.0 / HALF)
@@ -310,24 +275,20 @@
                 entering[side, part, high : low + PAIR, lanes] = jnp.where(first, zero, pair)
                 entering[side, part, low : low + PAIR, rest] = jnp.zeros((PAIR, PAIR), BF)
     for side in range(2):
-        for i in range(chunks):
-            for one in load(side, i):
-                one.wait()
-            for t in WEIGHT_STAGES[side * chunks + i]:
-                fetch(0, t).start()
-                fetch(1, t).start()
-            for part in range(i * per, (i + 1) * per):
-                c = slice(part * WIDE, (part + 1) * WIDE)
-                across = mm_nt(rin_buf[side, :, c], entering[side, part])
-                wkv = out_buf[side, :, c].astype(F32) + across
-                wkv_buf[side, :, c] = wkv
-                gated[side, :, c] = (wkv * wkv).astype(BF)
+        out_ref, rin_ref, _ = results[side]
+        for part in range(parts):
+            c = slice(part * WIDE, (part + 1) * WIDE)
+            across = mm_nt(rin_ref[:, c], entering[side, part])
+            wkv = out_ref[:, c].astype(F32) + across
+            wkv_buf[side, :, c] = wkv
+            gated[side, :, c] = (wkv * wkv).astype(BF)
     for side in range(2):
+        sg_ref = results[side][2]
         for part in range(parts):
             c = slice(part * WIDE, (part + 1) * WIDE)
             var = mm(gated[side, :, c], share)
             gated[side, :, c] = (
-                wkv_buf[side, :, c] * lax.rsqrt(var + EPS) * sg_buf[side, :, c].astype(F32)
+                wkv_buf[side, :, c] * lax.rsqrt(var + EPS) * sg_ref[:, c].astype(F32)
             ).astype(BF)
 
     def project(t, carry):
@@ -387,10 +348,9 @@
     return pl.pallas_call(
         local_kernel,
         in_specs=[pl.BlockSpec(memory_space=pltpu.SMEM)] + [vmem_block] * 2 + [any_block] * 5,
-        out_specs=[any_block] * 3,
-        out_shape=[pltpu.HBM(block, BF)] * 3,
-        scratch_shapes=[pltpu.VMEM(block, BF)] * 8
-        + [pltpu.SemaphoreType.DMA((5, chunks)), pltpu.SemaphoreType.DMA((3, chunks))],
+        out_specs=[vmem_block] * 3,
+        out_shape=[jax.ShapeDtypeStruct(block, BF)] * 3,
+        scratch_shapes=[pltpu.VMEM(block, BF)] * 5 + [pltpu.SemaphoreType.DMA((5, chunks))],
         compiler_params=params(limit=32 << 20),
         cost_estimate=pl.CostEstimate(flops=8 << 30, bytes_accessed=4 << 20, transcendentals=2 << 20),
         name="local",
@@ -398,7 +358,6 @@
 
 
 def call_scan(msg, anchor):
-    anchor = in_hbm(anchor)
     return pl.pallas_call(
         scan_kernel,
         in_specs=[pl.BlockSpec(memory_space=pltpu.VMEM), pl.BlockSpec(memory_space=pl.ANY)],
@@ -411,25 +370,21 @@
 def call_finish(core, entering, mine, other, weight, other_weight):
     half, cols = weight.shape
     tokens = mine[0].shape[0]
-    chunks, tiles = 2, 8
-    mine, other = ([in_hbm(x) for x in part] for part in (mine, other))
+    tiles = 8
     any_block = pl.BlockSpec(memory_space=pl.ANY)
     return pl.pallas_call(
         finish_kernel,
-        in_specs=[pl.BlockSpec(memory_space=pltpu.SMEM), pl.BlockSpec(memory_space=pltpu.VMEM)]
-        + [any_block] * 8,
+        in_specs=[pl.BlockSpec(memory_space=pltpu.SMEM)]
+        + [pl.BlockSpec(memory_space=pltpu.VMEM)] * 7
+        + [any_block] * 2,
         out_specs=any_block,
         out_shape=jax.ShapeDtypeStruct((tokens, cols), BF),
         scratch_shapes=[
-            pltpu.VMEM((2, tokens, half), BF),
-            pltpu.VMEM((2, tokens, half), BF),
-            pltpu.VMEM((2, tokens, half), BF),
             pltpu.VMEM((2, half, cols), BF),
             pltpu.VMEM((2, tokens, half), F32),
             pltpu.VMEM((2, half // WIDE, WIDE, WIDE), BF),
             pltpu.VMEM((2, tokens, half), BF),
             pltpu.VMEM((tokens, cols), BF),
-            pltpu.SemaphoreType.DMA((3, 2, chunks)),
             pltpu.SemaphoreType.DMA((2, tiles)),
             pltpu.SemaphoreType.DMA((tiles,)),
         ],

time: 53.2 us -> 52.1 us (0.979)
  Pallas kernels: 25.3 us -> 22.7 us
  waiting for transfers between devices: 10.3 us -> 11.8 us
    pallas_call x2, Pallas kernels: 11.3 us -> 9.7 us  [call_local(): pl.pallas_call(local_kernel, in_specs=[pl.BlockSpec(memory_space=pltpu.SM...]
    pallas_call x1, Pallas kernels: 9.63 us -> 8.55 us  [call_finish(): pl.pallas_call(finish_kernel, in_specs=[pl.BlockSpec(memory_space=pltpu.S...]
    all_to_all x1, waiting for transfers between devices: 4.83 us -> 5.64 us  [shards(): msg = lax.all_to_all(msg, SEQ_HEAD, split_axis=0, concat_axis=0, tiled=True)]
    all_to_all x1, waiting for transfers between devices: 5.41 us -> 6.19 us  [shards(): lax.all_to_all(entering, SEQ_HEAD, split_axis=0, concat_axis=0, tiled=True)]
  transfers between devices with their start and end apart: 5 -> 5, of which waited for: 2 -> 2; matrix products, arithmetic and copies ran while one was open for 0% -> 0% of each run, Pallas kernels for 30% -> 27%
where the time goes in v4:
time: 52.1 us; the launch traced here: 51.8 us
  Pallas kernels  22.7 us (44%)
  starting transfers between devices  17.2 us (33%)
  waiting for transfers between devices  11.8 us (23%)
    all_to_all x1, starting transfers between devices, shards(): msg = lax.all_to_all(msg, SEQ_HEAD, split_axis=0, concat_axis=0, tiled=True)  10.2 us
    pallas_call x2, Pallas kernels, call_local(): pl.pallas_call(local_kernel, in_specs=[pl.BlockSpec(memory_space=pltpu.SM...  9.7 us
    pallas_call x1, Pallas kernels, call_finish(): pl.pallas_call(finish_kernel, in_specs=[pl.BlockSpec(memory_space=pltpu.S...  8.55 us
    all_to_all x1, waiting for transfers between devices, shards(): lax.all_to_all(entering, SEQ_HEAD, split_axis=0, concat_axis=0, tiled=True)  6.19 us
    all_to_all x1, waiting for transfers between devices, shards(): msg = lax.all_to_all(msg, SEQ_HEAD, split_axis=0, concat_axis=0, tiled=True)  5.64 us
    all_to_all x1, starting transfers between devices, shards(): lax.all_to_all(entering, SEQ_HEAD, split_axis=0, concat_axis=0, tiled=True)  4.4 us
    pallas_call x1, Pallas kernels, call_state(): pl.pallas_call(state_kernel, in_specs=[any_block] * 3, out_specs=any_bloc...  3.41 us
    ppermute x1, starting transfers between devices, shards(): other_weight = lax.ppermute(weight, 'head', swap)  1.38 us
  transfers between devices with their start and end apart: 5, of which 2 were waited for; matrix products, arithmetic and copies ran while one was open for 0% of the time, Pallas kernels for 27%

profile of v4, /device:TPU:1, one launch (start us, length us, event | category | flops | bytes accessed | tf_op | source)
XLA Modules:
  0.0 51.8 jit_solution(8876917249832441455)
XLA Ops:
  0.0 0.0 copy-start
  0.0 0.0 copy-start.1
  0.0 1.4 %collective-permute-start.2 = (bf16[1024,4096]{1,0:T(8,128)(2,1)}, bf16[1024,4096]{1,0:T(8,128)(2,1)}, u32[]{:S(2)}, u32[]{:S(2)}) collective-permute-start(bf16[1024,4096]{1,0:T(8,128)(2,1)} %w1_hbm.1), channel_id=1, source_target_pairs={{0,1},{1,0},{2,3},{3,2},{4,5},{5,4},{6,7},{7,6},{8,9},{9,8},{10,11... | collective-permute-start | bytes 25165832 | tf_op jit(solution)/shard_map/ppermute | solution.py:402
  1.4 3.4 %state.1 = bf16[128,5,2,128]{3,2,1,0:T(2,128)(2,1)} custom-call(bf16[256,2048]{1,0:T(8,128)(2,1)} %k_hbm.5, bf16[256,2048]{1,0:T(8,128)(2,1)} %v_hbm.5, bf16[256,2048]{1,0:T(8,128)(2,1)} %w_hbm.5), custom_call_target="tpu_custom_call" | custom-call | flops 4294967296 | bytes 4194304 | tf_op jit(solution)/shard_map/state/pallas_call | solution.py:325
  4.8 10.2 %all-to-all-start = ((bf16[128,5,2,128]{3,2,1,0:T(2,128)(2,1)}), bf16[128,5,2,128]{3,2,1,0:T(2,128)(2,1)S(1)}, u32[]{:S(2)}, u32[]{:S(2)}) async-start(bf16[128,5,2,128]{3,2,1,0:T(2,128)(2,1)} %state.1), calls=%async_computation | async-start | bytes 655360 | tf_op jit(solution)/shard_map/all_to_all | solution.py:404
  15.0 0.0 copy-done
  15.0 0.0 copy-done.1
  15.1 4.9 %local.2 = (bf16[256,1024]{1,0:T(8,128)(2,1)S(1)}, bf16[256,1024]{1,0:T(8,128)(2,1)S(1)}, bf16[256,1024]{1,0:T(8,128)(2,1)S(1)}) custom-call(s32[1]{0:T(128)} %bitcast.h_ref.c_ref, f32[16,64]{1,0:T(8,128)S(1)} %copy-done, f32[1,1024]{1,0:T(1,128)S(1)} %bitcast.4, bf16[256,2048]{1,0:T(8,128)(2,1)} %r_hbm.3, bf16[256,2048]{1,0:T(8,128)(2,1)} %k_hbm.5, ...), custom_call_target="tpu_custom_call" | custom-call | flops 8589934592 | bytes 4194304 | tf_op jit(solution)/shard_map/local/pallas_call | solution.py:348
  19.9 1.1 %collective-permute-start.1 = (f32[1,1024]{1,0:T(1,128)S(1)}, f32[1,1024]{1,0:T(1,128)S(1)}, u32[]{:S(2)}, u32[]{:S(2)}) collective-permute-start(f32[1,1024]{1,0:T(1,128)S(1)} %bitcast.5), channel_id=1, source_target_pairs={{0,1},{1,0},{2,3},{3,2},{4,5},{5,4},{6,7},{7,6},{8,9},{9,8},{10,11... | collective-permute-start | bytes 12296 | tf_op jit(solution)/shard_map/ppermute | solution.py:409
  21.1 0.1 collective-permute-start
  21.2 5.6 %all-to-all-done.msg_ref = bf16[128,5,2,128]{3,2,1,0:T(2,128)(2,1)S(1)} async-done(((bf16[128,5,2,128]{3,2,1,0:T(2,128)(2,1)}), bf16[128,5,2,128]{3,2,1,0:T(2,128)(2,1)S(1)}, u32[]{:S(2)}, u32[]{:S(2)}) %all-to-all-start) | async-done | bytes 327712 | tf_op jit(solution)/shard_map/all_to_all | solution.py:404
  26.8 1.0 %scan.1 = bf16[128,8,128]{2,1,0:T(8,128)(2,1)} custom-call(bf16[128,5,2,128]{3,2,1,0:T(2,128)(2,1)S(1)} %all-to-all-done.msg_ref, bf16[256,1024]{1,0:T(8,128)(2,1)S(1)} %get-tuple-element.13.after_ref.mine_rin), custom_call_target="tpu_custom_call" | custom-call | tf_op jit(solution)/shard_map/scan/pallas_call | solution.py:361
  27.8 4.4 %all-to-all-start.1 = ((bf16[128,8,128]{2,1,0:T(8,128)(2,1)}), bf16[128,8,128]{2,1,0:T(8,128)(2,1)S(1)}, u32[]{:S(2)}, u32[]{:S(2)}) async-start(bf16[128,8,128]{2,1,0:T(8,128)(2,1)} %scan.1), calls=%async_computation.1 | async-start | bytes 524288 | tf_op jit(solution)/shard_map/all_to_all | solution.py:407
  32.2 0.0 collective-permute-done.1.gain_ref
  32.2 0.0 collective-permute-done.u_ref
  32.2 4.9 %local.3 = (bf16[256,1024]{1,0:T(8,128)(2,1)S(1)}, bf16[256,1024]{1,0:T(8,128)(2,1)S(1)}, bf16[256,1024]{1,0:T(8,128)(2,1)S(1)}) custom-call(s32[1]{0:T(128)S(6)} %sub.3.h_ref, f32[16,64]{1,0:T(8,128)S(1)} %collective-permute-done.u_ref, f32[1,1024]{1,0:T(1,128)S(1)} %collective-permute-done.1.gain_ref, bf16[256,2048]{1,0:T(8,128)(2,1)} %r_hbm.3, ...), custom_call_target="tpu_custom_call" | custom-call | flops 8589934592 | bytes 4194304 | tf_op jit(solution)/shard_map/local/pallas_call | solution.py:348
  37.1 6.2 %all-to-all-done.1 = bf16[128,8,128]{2,1,0:T(8,128)(2,1)S(1)} async-done(((bf16[128,8,128]{2,1,0:T(8,128)(2,1)}), bf16[128,8,128]{2,1,0:T(8,128)(2,1)S(1)}, u32[]{:S(2)}, u32[]{:S(2)}) %all-to-all-start.1) | async-done | bytes 262176 | tf_op jit(solution)/shard_map/all_to_all | solution.py:407
  43.3 0.0 collective-permute-done.2.w2_hbm
  43.3 8.5 %finish.1 = bf16[256,4096]{1,0:T(8,128)(2,1)} custom-call(s32[1]{0:T(128)} %bitcast.h_ref.c_ref, bf16[16,64,128]{2,1,0:T(8,128)(2,1)S(1)} %bitcast.3, bf16[256,1024]{1,0:T(8,128)(2,1)S(1)} %get-tuple-element.14.mine_out, bf16[256,1024]{1,0:T(8,128)(2,1)S(1)} %get-tuple-element.13.after_ref.mine_rin, bf16[256,1024]{1,0:T(8,128)(2,1)S(1)} %get-tuple-element.15.mine_sg, ...), custom_call_target="tpu_custom_call" | custom-call | tf_op jit(solution)/shard_map/finish/pallas_call | solution.py:375
Async XLA Ops:
  0.0 15.0 %copy-start = (f32[16,64]{1,0:T(8,128)S(1)}, f32[16,64]{1,0:T(8,128)}, u32[]{:S(2)}) copy-start(f32[16,64]{1,0:T(8,128)} %u_ref.1) | copy-start | bytes 12292
  0.0 15.0 %copy-start.1 = (f32[1024]{0:T(1024)S(1)}, f32[1024]{0:T(1024)}, u32[]{:S(2)}) copy-start(f32[1024]{0:T(1024)} %param.14) | copy-start | bytes 12292
  0.0 43.3 %collective-permute-start.2 = (bf16[1024,4096]{1,0:T(8,128)(2,1)}, bf16[1024,4096]{1,0:T(8,128)(2,1)}, u32[]{:S(2)}, u32[]{:S(2)}) collective-permute-start(bf16[1024,4096]{1,0:T(8,128)(2,1)} %w1_hbm.1), channel_id=1, source_target_pairs={{0,1},{1,0},{2,3},{3,2},{4,5},{5,4},{6,7},{7,6},{8,9},{9,8},{10,11... | collective-permute-start | bytes 25165832 | tf_op jit(solution)/shard_map/ppermute | solution.py:402
  4.8 22.0 %all-to-all-start = ((bf16[128,5,2,128]{3,2,1,0:T(2,128)(2,1)}), bf16[128,5,2,128]{3,2,1,0:T(2,128)(2,1)S(1)}, u32[]{:S(2)}, u32[]{:S(2)}) async-start(bf16[128,5,2,128]{3,2,1,0:T(2,128)(2,1)} %state.1), calls=%async_computation | async-start | bytes 655360 | tf_op jit(solution)/shard_map/all_to_all | solution.py:404
  19.9 12.3 %collective-permute-start.1 = (f32[1,1024]{1,0:T(1,128)S(1)}, f32[1,1024]{1,0:T(1,128)S(1)}, u32[]{:S(2)}, u32[]{:S(2)}) collective-permute-start(f32[1,1024]{1,0:T(1,128)S(1)} %bitcast.5), channel_id=1, source_target_pairs={{0,1},{1,0},{2,3},{3,2},{4,5},{5,4},{6,7},{7,6},{8,9},{9,8},{10,11... | collective-permute-start | bytes 12296 | tf_op jit(solution)/shard_map/ppermute | solution.py:409
  21.1 11.2 %collective-permute-start = (f32[16,64]{1,0:T(8,128)S(1)}, f32[16,64]{1,0:T(8,128)S(1)}, u32[]{:S(2)}, u32[]{:S(2)}) collective-permute-start(f32[16,64]{1,0:T(8,128)S(1)} %copy-done), channel_id=1, source_target_pairs={{0,1},{1,0},{2,3},{3,2},{4,5},{5,4},{6,7},{7,6},{8,9},{9,8},{10,11... | collective-permute-start | bytes 12296 | tf_op jit(solution)/shard_map/ppermute | solution.py:409
  27.8 15.5 %all-to-all-start.1 = ((bf16[128,8,128]{2,1,0:T(8,128)(2,1)}), bf16[128,8,128]{2,1,0:T(8,128)(2,1)S(1)}, u32[]{:S(2)}, u32[]{:S(2)}) async-start(bf16[128,8,128]{2,1,0:T(8,128)(2,1)} %scan.1), calls=%async_computation.1 | async-start | bytes 524288 | tf_op jit(solution)/shard_map/all_to_all | solution.py:407

commit v5 on v4

--- a/solution.py
+++ b/solution.py
@@ -54,7 +54,9 @@
 
 
 def centred(v):
-    return (v.astype(F32) - mm(v, head_ones(1.0 / HALF))).astype(BF)
+    row, col = grid2(WIDE, WIDE)
+    less_mean = jnp.where(row == col, 1.0, 0.0) - jnp.where(row // HALF == col // HALF, 1.0 / HALF, 0.0)
+    return mm(v, less_mean.astype(BF)).astype(BF)
 
 
 def state_kernel(k_hbm, v_hbm, w_hbm, msg_hbm, k_buf, v_buf, w_buf, msg_buf, in_sems, out_sems):
@@ -93,7 +95,7 @@
             s = slice(part * WIDE, (part + 1) * WIDE)
             rate = decay_rate(w_buf[:, s])
             after = mm(later, rate)
-            key_end = k_buf[:, s] * jnp.exp2(after).astype(BF)
+            key_end = (k_buf[:, s].astype(F32) * jnp.exp2(after)).astype(BF)
             total = after[0:1] - rate[0:1].astype(F32)
             state = mm_tn(v_buf[:, s], key_end)
             tot_hi, tot_lo = two_parts(total)
@@ -182,17 +184,18 @@
         k = k_ref[:, c]
         v = centred(v_ref[:, c])
         mid0, end0, mid1 = cum[63:64], cum[127:128], cum[191:192]
-        r0 = r[:BLOCK] * jnp.exp2(before[:BLOCK] - mid0).astype(BF)
-        k0 = k[:BLOCK] * jnp.exp2(mid0 - cum[:BLOCK]).astype(BF)
-        r1 = r[BLOCK:] * jnp.exp2(before[BLOCK:] - mid1).astype(BF)
-        k1 = k[BLOCK:] * jnp.exp2(mid1 - cum[BLOCK:]).astype(BF)
-        r1c = r[BLOCK:] * jnp.exp2(before[BLOCK:] - end0).astype(BF)
-        k0c = k[:BLOCK] * jnp.exp2(end0 - cum[:BLOCK]).astype(BF)
-        rin_ref[:BLOCK, c] = r[:BLOCK] * jnp.exp2(before[:BLOCK]).astype(BF)
-        rin_ref[BLOCK:, c] = r[BLOCK:] * jnp.exp2(before[BLOCK:]).astype(BF)
+        rf, kf = r.astype(F32), k.astype(F32)
+        r0 = (rf[:BLOCK] * jnp.exp2(before[:BLOCK] - mid0)).astype(BF)
+        k0 = (kf[:BLOCK] * jnp.exp2(mid0 - cum[:BLOCK])).astype(BF)
+        r1 = (rf[BLOCK:] * jnp.exp2(before[BLOCK:] - mid1)).astype(BF)
+        k1 = (kf[BLOCK:] * jnp.exp2(mid1 - cum[BLOCK:])).astype(BF)
+        r1c = (rf[BLOCK:] * jnp.exp2(before[BLOCK:] - end0)).astype(BF)
+        k0c = (kf[:BLOCK] * jnp.exp2(end0 - cum[:BLOCK])).astype(BF)
+        rin_ref[:BLOCK, c] = (rf[:BLOCK] * jnp.exp2(before[:BLOCK])).astype(BF)
+        rin_ref[BLOCK:, c] = (rf[BLOCK:] * jnp.exp2(before[BLOCK:])).astype(BF)
         heads = range(at // HALF, (at + WIDE) // HALF)
         u = jnp.concatenate([u_ref[h : h + 1] for h in heads], axis=1)
-        bonus = (r.astype(F32) * u * k.astype(F32)).astype(BF)
+        bonus = (rf * u * kf).astype(BF)
         own = mm(bonus, head_ones(1.0)) * v.astype(F32)
         for p in range(WIDE // PAIR):
             s = slice(p * PAIR, (p + 1) * PAIR)

time: 52.1 us -> 52.1 us (level)
  no operation moved by 1% of the time
where the time goes in v5:
time: 52.1 us; the launch traced here: 51.8 us
  Pallas kernels  22.6 us (43%)
  starting transfers between devices  17.3 us (33%)
  waiting for transfers between devices  11.9 us (23%)
    all_to_all x1, starting transfers between devices, shards(): msg = lax.all_to_all(msg, SEQ_HEAD, split_axis=0, concat_axis=0, tiled=True)  10.2 us
    pallas_call x2, Pallas kernels, call_local(): pl.pallas_call(local_kernel, in_specs=[pl.BlockSpec(memory_space=pltpu.SM...  9.67 us
    pallas_call x1, Pallas kernels, call_finish(): pl.pallas_call(finish_kernel, in_specs=[pl.BlockSpec(memory_space=pltpu.S...  8.55 us
    all_to_all x1, waiting for transfers between devices, shards(): lax.all_to_all(entering, SEQ_HEAD, split_axis=0, concat_axis=0, tiled=True)  6.21 us
    all_to_all x1, waiting for transfers between devices, shards(): msg = lax.all_to_all(msg, SEQ_HEAD, split_axis=0, concat_axis=0, tiled=True)  5.66 us
    all_to_all x1, starting transfers between devices, shards(): lax.all_to_all(entering, SEQ_HEAD, split_axis=0, concat_axis=0, tiled=True)  4.4 us
    pallas_call x1, Pallas kernels, call_state(): pl.pallas_call(state_kernel, in_specs=[any_block] * 3, out_specs=any_bloc...  3.41 us
    ppermute x1, starting transfers between devices, shards(): other_weight = lax.ppermute(weight, 'head', swap)  1.38 us
  transfers between devices with their start and end apart: 5, of which 2 were waited for; matrix products, arithmetic and copies ran while one was open for 0% of the time, Pallas kernels for 27%

profile of v5, /device:TPU:1, one launch (start us, length us, event | category | flops | bytes accessed | tf_op | source)
XLA Modules:
  0.0 51.8 jit_solution(530530152307693753)
XLA Ops:
  0.0 0.0 copy-start
  0.0 0.0 copy-start.1
  0.0 1.4 %collective-permute-start.2 = (bf16[1024,4096]{1,0:T(8,128)(2,1)}, bf16[1024,4096]{1,0:T(8,128)(2,1)}, u32[]{:S(2)}, u32[]{:S(2)}) collective-permute-start(bf16[1024,4096]{1,0:T(8,128)(2,1)} %w1_hbm.1), channel_id=1, source_target_pairs={{0,1},{1,0},{2,3},{3,2},{4,5},{5,4},{6,7},{7,6},{8,9},{9,8},{10,11... | collective-permute-start | bytes 25165832 | tf_op jit(solution)/shard_map/ppermute | solution.py:405
  1.4 3.4 %state.1 = bf16[128,5,2,128]{3,2,1,0:T(2,128)(2,1)} custom-call(bf16[256,2048]{1,0:T(8,128)(2,1)} %k_hbm.5, bf16[256,2048]{1,0:T(8,128)(2,1)} %v_hbm.5, bf16[256,2048]{1,0:T(8,128)(2,1)} %w_hbm.5), custom_call_target="tpu_custom_call" | custom-call | flops 4294967296 | bytes 4194304 | tf_op jit(solution)/shard_map/state/pallas_call | solution.py:328
  4.8 10.2 %all-to-all-start = ((bf16[128,5,2,128]{3,2,1,0:T(2,128)(2,1)}), bf16[128,5,2,128]{3,2,1,0:T(2,128)(2,1)S(1)}, u32[]{:S(2)}, u32[]{:S(2)}) async-start(bf16[128,5,2,128]{3,2,1,0:T(2,128)(2,1)} %state.1), calls=%async_computation | async-start | bytes 655360 | tf_op jit(solution)/shard_map/all_to_all | solution.py:407
  15.0 0.0 copy-done
  15.0 0.0 copy-done.1
  15.1 4.8 %local.2 = (bf16[256,1024]{1,0:T(8,128)(2,1)S(1)}, bf16[256,1024]{1,0:T(8,128)(2,1)S(1)}, bf16[256,1024]{1,0:T(8,128)(2,1)S(1)}) custom-call(s32[1]{0:T(128)} %bitcast.h_ref.c_ref, f32[16,64]{1,0:T(8,128)S(1)} %copy-done, f32[1,1024]{1,0:T(1,128)S(1)} %bitcast.4, bf16[256,2048]{1,0:T(8,128)(2,1)} %r_hbm.3, bf16[256,2048]{1,0:T(8,128)(2,1)} %k_hbm.5, ...), custom_call_target="tpu_custom_call" | custom-call | flops 8589934592 | bytes 4194304 | tf_op jit(solution)/shard_map/local/pallas_call | solution.py:351
  19.9 1.2 %collective-permute-start.1 = (f32[1,1024]{1,0:T(1,128)S(1)}, f32[1,1024]{1,0:T(1,128)S(1)}, u32[]{:S(2)}, u32[]{:S(2)}) collective-permute-start(f32[1,1024]{1,0:T(1,128)S(1)} %bitcast.5), channel_id=1, source_target_pairs={{0,1},{1,0},{2,3},{3,2},{4,5},{5,4},{6,7},{7,6},{8,9},{9,8},{10,11... | collective-permute-start | bytes 12296 | tf_op jit(solution)/shard_map/ppermute | solution.py:412
  21.1 0.1 collective-permute-start
  21.1 5.7 %all-to-all-done.msg_ref = bf16[128,5,2,128]{3,2,1,0:T(2,128)(2,1)S(1)} async-done(((bf16[128,5,2,128]{3,2,1,0:T(2,128)(2,1)}), bf16[128,5,2,128]{3,2,1,0:T(2,128)(2,1)S(1)}, u32[]{:S(2)}, u32[]{:S(2)}) %all-to-all-start) | async-done | bytes 327712 | tf_op jit(solution)/shard_map/all_to_all | solution.py:407
  26.8 1.0 %scan.1 = bf16[128,8,128]{2,1,0:T(8,128)(2,1)} custom-call(bf16[128,5,2,128]{3,2,1,0:T(2,128)(2,1)S(1)} %all-to-all-done.msg_ref, bf16[256,1024]{1,0:T(8,128)(2,1)S(1)} %get-tuple-element.13.after_ref.mine_rin), custom_call_target="tpu_custom_call" | custom-call | tf_op jit(solution)/shard_map/scan/pallas_call | solution.py:364
  27.8 4.4 %all-to-all-start.1 = ((bf16[128,8,128]{2,1,0:T(8,128)(2,1)}), bf16[128,8,128]{2,1,0:T(8,128)(2,1)S(1)}, u32[]{:S(2)}, u32[]{:S(2)}) async-start(bf16[128,8,128]{2,1,0:T(8,128)(2,1)} %scan.1), calls=%async_computation.1 | async-start | bytes 524288 | tf_op jit(solution)/shard_map/all_to_all | solution.py:410
  32.2 0.0 collective-permute-done.1.gain_ref
  32.2 0.0 collective-permute-done.u_ref
  32.2 4.8 %local.3 = (bf16[256,1024]{1,0:T(8,128)(2,1)S(1)}, bf16[256,1024]{1,0:T(8,128)(2,1)S(1)}, bf16[256,1024]{1,0:T(8,128)(2,1)S(1)}) custom-call(s32[1]{0:T(128)S(6)} %sub.3.h_ref, f32[16,64]{1,0:T(8,128)S(1)} %collective-permute-done.u_ref, f32[1,1024]{1,0:T(1,128)S(1)} %collective-permute-done.1.gain_ref, bf16[256,2048]{1,0:T(8,128)(2,1)} %r_hbm.3, ...), custom_call_target="tpu_custom_call" | custom-call | flops 8589934592 | bytes 4194304 | tf_op jit(solution)/shard_map/local/pallas_call | solution.py:351
  37.1 6.2 %all-to-all-done.1 = bf16[128,8,128]{2,1,0:T(8,128)(2,1)S(1)} async-done(((bf16[128,8,128]{2,1,0:T(8,128)(2,1)}), bf16[128,8,128]{2,1,0:T(8,128)(2,1)S(1)}, u32[]{:S(2)}, u32[]{:S(2)}) %all-to-all-start.1) | async-done | bytes 262176 | tf_op jit(solution)/shard_map/all_to_all | solution.py:410
  43.3 0.0 collective-permute-done.2.w2_hbm
  43.3 8.6 %finish.1 = bf16[256,4096]{1,0:T(8,128)(2,1)} custom-call(s32[1]{0:T(128)} %bitcast.h_ref.c_ref, bf16[16,64,128]{2,1,0:T(8,128)(2,1)S(1)} %bitcast.3, bf16[256,1024]{1,0:T(8,128)(2,1)S(1)} %get-tuple-element.14.mine_out, bf16[256,1024]{1,0:T(8,128)(2,1)S(1)} %get-tuple-element.13.after_ref.mine_rin, bf16[256,1024]{1,0:T(8,128)(2,1)S(1)} %get-tuple-element.15.mine_sg, ...), custom_call_target="tpu_custom_call" | custom-call | tf_op jit(solution)/shard_map/finish/pallas_call | solution.py:378
Async XLA Ops:
  0.0 15.0 %copy-start = (f32[16,64]{1,0:T(8,128)S(1)}, f32[16,64]{1,0:T(8,128)}, u32[]{:S(2)}) copy-start(f32[16,64]{1,0:T(8,128)} %u_ref.1) | copy-start | bytes 12292
  0.0 15.0 %copy-start.1 = (f32[1024]{0:T(1024)S(1)}, f32[1024]{0:T(1024)}, u32[]{:S(2)}) copy-start(f32[1024]{0:T(1024)} %param.14) | copy-start | bytes 12292
  0.0 43.3 %collective-permute-start.2 = (bf16[1024,4096]{1,0:T(8,128)(2,1)}, bf16[1024,4096]{1,0:T(8,128)(2,1)}, u32[]{:S(2)}, u32[]{:S(2)}) collective-permute-start(bf16[1024,4096]{1,0:T(8,128)(2,1)} %w1_hbm.1), channel_id=1, source_target_pairs={{0,1},{1,0},{2,3},{3,2},{4,5},{5,4},{6,7},{7,6},{8,9},{9,8},{10,11... | collective-permute-start | bytes 25165832 | tf_op jit(solution)/shard_map/ppermute | solution.py:405
  4.8 22.0 %all-to-all-start = ((bf16[128,5,2,128]{3,2,1,0:T(2,128)(2,1)}), bf16[128,5,2,128]{3,2,1,0:T(2,128)(2,1)S(1)}, u32[]{:S(2)}, u32[]{:S(2)}) async-start(bf16[128,5,2,128]{3,2,1,0:T(2,128)(2,1)} %state.1), calls=%async_computation | async-start | bytes 655360 | tf_op jit(solution)/shard_map/all_to_all | solution.py:407
  19.9 12.3 %collective-permute-start.1 = (f32[1,1024]{1,0:T(1,128)S(1)}, f32[1,1024]{1,0:T(1,128)S(1)}, u32[]{:S(2)}, u32[]{:S(2)}) collective-permute-start(f32[1,1024]{1,0:T(1,128)S(1)} %bitcast.5), channel_id=1, source_target_pairs={{0,1},{1,0},{2,3},{3,2},{4,5},{5,4},{6,7},{7,6},{8,9},{9,8},{10,11... | collective-permute-start | bytes 12296 | tf_op jit(solution)/shard_map/ppermute | solution.py:412
  21.1 11.2 %collective-permute-start = (f32[16,64]{1,0:T(8,128)S(1)}, f32[16,64]{1,0:T(8,128)S(1)}, u32[]{:S(2)}, u32[]{:S(2)}) collective-permute-start(f32[16,64]{1,0:T(8,128)S(1)} %copy-done), channel_id=1, source_target_pairs={{0,1},{1,0},{2,3},{3,2},{4,5},{5,4},{6,7},{7,6},{8,9},{9,8},{10,11... | collective-permute-start | bytes 12296 | tf_op jit(solution)/shard_map/ppermute | solution.py:412
  27.8 15.5 %all-to-all-start.1 = ((bf16[128,8,128]{2,1,0:T(8,128)(2,1)}), bf16[128,8,128]{2,1,0:T(8,128)(2,1)S(1)}, u32[]{:S(2)}, u32[]{:S(2)}) async-start(bf16[128,8,128]{2,1,0:T(8,128)(2,1)} %scan.1), calls=%async_computation.1 | async-start | bytes 524288 | tf_op jit(solution)/shard_map/all_to_all | solution.py:410

commit v6 on v5

--- a/solution.py
+++ b/solution.py
@@ -15,7 +15,7 @@
 EPS = 1e-05
 LOG2E = 1.4426950408889634
 LOG2LOG2E = 0.5287663729448977
-TILES_AHEAD = 4
+TILES_AHEAD = 5
 BF = jnp.bfloat16
 F32 = jnp.float32
 
@@ -214,14 +214,24 @@
             compute(part)
 
 
-def scan_kernel(msg_ref, after_ref, out_ref):
+def scan_kernel(msg_ref, after_ref, out_hbm, out_ref, sems):
     groups = msg_ref.shape[0]
+    pieces = sems.shape[0]
+    per = groups // pieces
+    stores = [
+        pltpu.make_async_copy(out_ref.at[pl.ds(i * per, per)], out_hbm.at[pl.ds(i * per, per)], sems.at[i])
+        for i in range(pieces)
+    ]
     state = jnp.zeros((8, PAIR), F32)
     for g in range(groups):
         logs = msg_ref[g, 4].astype(F32)
         out_ref[g] = state.astype(BF)
+        if g % per == per - 1:
+            stores[g // per].start()
         decay = jnp.exp2(logs[0:1] + logs[1:2])
         state = state * decay + msg_ref[g, 0:4].reshape(8, PAIR).astype(F32)
+    for one in stores:
+        one.wait()
 
 
 def finish_kernel(
@@ -361,10 +371,13 @@
 
 
 def call_scan(msg, anchor):
+    shape = (msg.shape[0], 8, PAIR)
     return pl.pallas_call(
         scan_kernel,
         in_specs=[pl.BlockSpec(memory_space=pltpu.VMEM), pl.BlockSpec(memory_space=pl.ANY)],
-        out_shape=jax.ShapeDtypeStruct((msg.shape[0], 8, PAIR), BF),
+        out_specs=pl.BlockSpec(memory_space=pl.ANY),
+        out_shape=pltpu.HBM(shape, BF),
+        scratch_shapes=[pltpu.VMEM(shape, BF), pltpu.SemaphoreType.DMA((4,))],
         compiler_params=params(limit=8 << 20),
         name="scan",
     )(msg, anchor)

time: 52.1 us -> 52 us (level)
  no operation moved by 1% of the time
where the time goes in v6:
time: 52 us; the launch traced here: 51.8 us
  Pallas kernels  22.6 us (43%)
  starting transfers between devices  17.3 us (33%)
  waiting for transfers between devices  11.9 us (23%)
    all_to_all x1, starting transfers between devices, shards(): msg = lax.all_to_all(msg, SEQ_HEAD, split_axis=0, concat_axis=0, tiled=True)  10.2 us
    pallas_call x2, Pallas kernels, call_local(): pl.pallas_call(local_kernel, in_specs=[pl.BlockSpec(memory_space=pltpu.SM...  9.67 us
    pallas_call x1, Pallas kernels, call_finish(): pl.pallas_call(finish_kernel, in_specs=[pl.BlockSpec(memory_space=pltpu.S...  8.54 us
    all_to_all x1, waiting for transfers between devices, shards(): lax.all_to_all(entering, SEQ_HEAD, split_axis=0, concat_axis=0, tiled=True)  6.21 us
    all_to_all x1, waiting for transfers between devices, shards(): msg = lax.all_to_all(msg, SEQ_HEAD, split_axis=0, concat_axis=0, tiled=True)  5.66 us
    all_to_all x1, starting transfers between devices, shards(): lax.all_to_all(entering, SEQ_HEAD, split_axis=0, concat_axis=0, tiled=True)  4.4 us
    pallas_call x1, Pallas kernels, call_state(): pl.pallas_call(state_kernel, in_specs=[any_block] * 3, out_specs=any_bloc...  3.41 us
    ppermute x1, starting transfers between devices, shards(): other_weight = lax.ppermute(weight, 'head', swap)  1.38 us
  transfers between devices with their start and end apart: 5, of which 2 were waited for; matrix products, arithmetic and copies ran while one was open for 0% of the time, Pallas kernels for 27%

profile of v6, /device:TPU:1, one launch (start us, length us, event | category | flops | bytes accessed | tf_op | source)
XLA Modules:
  0.0 51.8 jit_solution(15631896436715393683)
XLA Ops:
  0.0 0.0 copy-start
  0.0 0.0 copy-start.1
  0.0 1.4 %collective-permute-start.2 = (bf16[1024,4096]{1,0:T(8,128)(2,1)}, bf16[1024,4096]{1,0:T(8,128)(2,1)}, u32[]{:S(2)}, u32[]{:S(2)}) collective-permute-start(bf16[1024,4096]{1,0:T(8,128)(2,1)} %w1_hbm.1), channel_id=1, source_target_pairs={{0,1},{1,0},{2,3},{3,2},{4,5},{5,4},{6,7},{7,6},{8,9},{9,8},{10,11... | collective-permute-start | bytes 25165832 | tf_op jit(solution)/shard_map/ppermute | solution.py:418
  1.4 3.4 %state.1 = bf16[128,5,2,128]{3,2,1,0:T(2,128)(2,1)} custom-call(bf16[256,2048]{1,0:T(8,128)(2,1)} %k_hbm.5, bf16[256,2048]{1,0:T(8,128)(2,1)} %v_hbm.5, bf16[256,2048]{1,0:T(8,128)(2,1)} %w_hbm.5), custom_call_target="tpu_custom_call" | custom-call | flops 4294967296 | bytes 4194304 | tf_op jit(solution)/shard_map/state/pallas_call | solution.py:338
  4.8 10.2 %all-to-all-start = ((bf16[128,5,2,128]{3,2,1,0:T(2,128)(2,1)}), bf16[128,5,2,128]{3,2,1,0:T(2,128)(2,1)S(1)}, u32[]{:S(2)}, u32[]{:S(2)}) async-start(bf16[128,5,2,128]{3,2,1,0:T(2,128)(2,1)} %state.1), calls=%async_computation | async-start | bytes 655360 | tf_op jit(solution)/shard_map/all_to_all | solution.py:420
  15.0 0.0 copy-done
  15.0 0.0 copy-done.1
  15.1 4.8 %local.2 = (bf16[256,1024]{1,0:T(8,128)(2,1)S(1)}, bf16[256,1024]{1,0:T(8,128)(2,1)S(1)}, bf16[256,1024]{1,0:T(8,128)(2,1)S(1)}) custom-call(s32[1]{0:T(128)} %bitcast.h_ref.c_ref, f32[16,64]{1,0:T(8,128)S(1)} %copy-done, f32[1,1024]{1,0:T(1,128)S(1)} %bitcast.4, bf16[256,2048]{1,0:T(8,128)(2,1)} %r_hbm.3, bf16[256,2048]{1,0:T(8,128)(2,1)} %k_hbm.5, ...), custom_call_target="tpu_custom_call" | custom-call | flops 8589934592 | bytes 4194304 | tf_op jit(solution)/shard_map/local/pallas_call | solution.py:361
  19.9 1.2 %collective-permute-start.1 = (f32[1,1024]{1,0:T(1,128)S(1)}, f32[1,1024]{1,0:T(1,128)S(1)}, u32[]{:S(2)}, u32[]{:S(2)}) collective-permute-start(f32[1,1024]{1,0:T(1,128)S(1)} %bitcast.5), channel_id=1, source_target_pairs={{0,1},{1,0},{2,3},{3,2},{4,5},{5,4},{6,7},{7,6},{8,9},{9,8},{10,11... | collective-permute-start | bytes 12296 | tf_op jit(solution)/shard_map/ppermute | solution.py:425
  21.1 0.1 collective-permute-start
  21.1 5.7 %all-to-all-done.msg_ref = bf16[128,5,2,128]{3,2,1,0:T(2,128)(2,1)S(1)} async-done(((bf16[128,5,2,128]{3,2,1,0:T(2,128)(2,1)}), bf16[128,5,2,128]{3,2,1,0:T(2,128)(2,1)S(1)}, u32[]{:S(2)}, u32[]{:S(2)}) %all-to-all-start) | async-done | bytes 327712 | tf_op jit(solution)/shard_map/all_to_all | solution.py:420
  26.8 1.0 %scan.1 = bf16[128,8,128]{2,1,0:T(8,128)(2,1)} custom-call(bf16[128,5,2,128]{3,2,1,0:T(2,128)(2,1)S(1)} %all-to-all-done.msg_ref, bf16[256,1024]{1,0:T(8,128)(2,1)S(1)} %get-tuple-element.13.after_ref.mine_rin), custom_call_target="tpu_custom_call" | custom-call | tf_op jit(solution)/shard_map/scan/pallas_call | solution.py:375
  27.8 4.4 %all-to-all-start.1 = ((bf16[128,8,128]{2,1,0:T(8,128)(2,1)}), bf16[128,8,128]{2,1,0:T(8,128)(2,1)S(1)}, u32[]{:S(2)}, u32[]{:S(2)}) async-start(bf16[128,8,128]{2,1,0:T(8,128)(2,1)} %scan.1), calls=%async_computation.1 | async-start | bytes 524288 | tf_op jit(solution)/shard_map/all_to_all | solution.py:423
  32.2 0.0 collective-permute-done.1.gain_ref
  32.2 0.0 collective-permute-done.u_ref
  32.2 4.8 %local.3 = (bf16[256,1024]{1,0:T(8,128)(2,1)S(1)}, bf16[256,1024]{1,0:T(8,128)(2,1)S(1)}, bf16[256,1024]{1,0:T(8,128)(2,1)S(1)}) custom-call(s32[1]{0:T(128)S(6)} %sub.3.h_ref, f32[16,64]{1,0:T(8,128)S(1)} %collective-permute-done.u_ref, f32[1,1024]{1,0:T(1,128)S(1)} %collective-permute-done.1.gain_ref, bf16[256,2048]{1,0:T(8,128)(2,1)} %r_hbm.3, ...), custom_call_target="tpu_custom_call" | custom-call | flops 8589934592 | bytes 4194304 | tf_op jit(solution)/shard_map/local/pallas_call | solution.py:361
  37.0 6.2 %all-to-all-done.1 = bf16[128,8,128]{2,1,0:T(8,128)(2,1)S(1)} async-done(((bf16[128,8,128]{2,1,0:T(8,128)(2,1)}), bf16[128,8,128]{2,1,0:T(8,128)(2,1)S(1)}, u32[]{:S(2)}, u32[]{:S(2)}) %all-to-all-start.1) | async-done | bytes 262176 | tf_op jit(solution)/shard_map/all_to_all | solution.py:423
  43.3 0.0 collective-permute-done.2.w2_hbm
  43.3 8.5 %finish.1 = bf16[256,4096]{1,0:T(8,128)(2,1)} custom-call(s32[1]{0:T(128)} %bitcast.h_ref.c_ref, bf16[16,64,128]{2,1,0:T(8,128)(2,1)S(1)} %bitcast.3, bf16[256,1024]{1,0:T(8,128)(2,1)S(1)} %get-tuple-element.14.mine_out, bf16[256,1024]{1,0:T(8,128)(2,1)S(1)} %get-tuple-element.13.after_ref.mine_rin, bf16[256,1024]{1,0:T(8,128)(2,1)S(1)} %get-tuple-element.15.mine_sg, ...), custom_call_target="tpu_custom_call" | custom-call | tf_op jit(solution)/shard_map/finish/pallas_call | solution.py:391
Async XLA Ops:
  0.0 15.0 %copy-start = (f32[16,64]{1,0:T(8,128)S(1)}, f32[16,64]{1,0:T(8,128)}, u32[]{:S(2)}) copy-start(f32[16,64]{1,0:T(8,128)} %u_ref.1) | copy-start | bytes 12292
  0.0 15.0 %copy-start.1 = (f32[1024]{0:T(1024)S(1)}, f32[1024]{0:T(1024)}, u32[]{:S(2)}) copy-start(f32[1024]{0:T(1024)} %param.14) | copy-start | bytes 12292
  0.0 43.3 %collective-permute-start.2 = (bf16[1024,4096]{1,0:T(8,128)(2,1)}, bf16[1024,4096]{1,0:T(8,128)(2,1)}, u32[]{:S(2)}, u32[]{:S(2)}) collective-permute-start(bf16[1024,4096]{1,0:T(8,128)(2,1)} %w1_hbm.1), channel_id=1, source_target_pairs={{0,1},{1,0},{2,3},{3,2},{4,5},{5,4},{6,7},{7,6},{8,9},{9,8},{10,11... | collective-permute-start | bytes 25165832 | tf_op jit(solution)/shard_map/ppermute | solution.py:418
  4.8 22.0 %all-to-all-start = ((bf16[128,5,2,128]{3,2,1,0:T(2,128)(2,1)}), bf16[128,5,2,128]{3,2,1,0:T(2,128)(2,1)S(1)}, u32[]{:S(2)}, u32[]{:S(2)}) async-start(bf16[128,5,2,128]{3,2,1,0:T(2,128)(2,1)} %state.1), calls=%async_computation | async-start | bytes 655360 | tf_op jit(solution)/shard_map/all_to_all | solution.py:420
  19.9 12.3 %collective-permute-start.1 = (f32[1,1024]{1,0:T(1,128)S(1)}, f32[1,1024]{1,0:T(1,128)S(1)}, u32[]{:S(2)}, u32[]{:S(2)}) collective-permute-start(f32[1,1024]{1,0:T(1,128)S(1)} %bitcast.5), channel_id=1, source_target_pairs={{0,1},{1,0},{2,3},{3,2},{4,5},{5,4},{6,7},{7,6},{8,9},{9,8},{10,11... | collective-permute-start | bytes 12296 | tf_op jit(solution)/shard_map/ppermute | solution.py:425
  21.1 11.1 %collective-permute-start = (f32[16,64]{1,0:T(8,128)S(1)}, f32[16,64]{1,0:T(8,128)S(1)}, u32[]{:S(2)}, u32[]{:S(2)}) collective-permute-start(f32[16,64]{1,0:T(8,128)S(1)} %copy-done), channel_id=1, source_target_pairs={{0,1},{1,0},{2,3},{3,2},{4,5},{5,4},{6,7},{7,6},{8,9},{9,8},{10,11... | collective-permute-start | bytes 12296 | tf_op jit(solution)/shard_map/ppermute | solution.py:425
  27.8 15.5 %all-to-all-start.1 = ((bf16[128,8,128]{2,1,0:T(8,128)(2,1)}), bf16[128,8,128]{2,1,0:T(8,128)(2,1)S(1)}, u32[]{:S(2)}, u32[]{:S(2)}) async-start(bf16[128,8,128]{2,1,0:T(8,128)(2,1)} %scan.1), calls=%async_computation.1 | async-start | bytes 524288 | tf_op jit(solution)/shard_map/all_to_all | solution.py:423

commit v7 on v6

--- a/solution.py
+++ b/solution.py
@@ -254,7 +254,7 @@
     w_sems,
     y_sems,
 ):
-    tiles = y_sems.shape[0]
+    tiles = y_sems.shape[0] - 1
     half = mine_out.shape[1]
     tile = y_buf.shape[1] // tiles
     parts = half // WIDE
@@ -269,6 +269,18 @@
 
     def store(t):
         return pltpu.make_async_copy(y_buf.at[:, cols(t)], y_hbm.at[:, cols(t)], y_sems.at[t])
+
+    def end_cols(q):
+        return pl.ds((tiles - 1) * tile + q * (tile // 2), tile // 2)
+
+    def fetch_end(j, q):
+        at, src = end_cols(q), (w1_hbm, w2_hbm)[j]
+        sem = w_sems.at[j, tiles - 1 + q]
+        return pltpu.make_async_copy(src.at[:, at], w_buf.at[j, :, at], sem)
+
+    def store_end(q):
+        at = end_cols(q)
+        return pltpu.make_async_copy(y_buf.at[:, at], y_hbm.at[:, at], y_sems.at[tiles - 1 + q])
 
     for t in range(TILES_AHEAD):
         fetch(0, t).start()
@@ -308,19 +320,33 @@
         fetch(0, t).wait()
         fetch(1, t).wait()
 
-        @pl.when(t + TILES_AHEAD < tiles)
+        @pl.when(t + TILES_AHEAD < tiles - 1)
         def _():
             fetch(0, t + TILES_AHEAD).start()
             fetch(1, t + TILES_AHEAD).start()
+
+        @pl.when(t + TILES_AHEAD == tiles - 1)
+        def _():
+            for q in range(2):
+                for j in range(2):
+                    fetch_end(j, q).start()
 
         y = mm(gated[0], w_buf[0, :, cols(t)]) + mm(gated[1], w_buf[1, :, cols(t)])
         y_buf[:, cols(t)] = y.astype(BF)
         store(t).start()
         return carry
 
-    lax.fori_loop(0, tiles, project, 0)
-    for t in range(tiles):
+    lax.fori_loop(0, tiles - 1, project, 0)
+    for q in range(2):
+        fetch_end(0, q).wait()
+        fetch_end(1, q).wait()
+        y = mm(gated[0], w_buf[0, :, end_cols(q)]) + mm(gated[1], w_buf[1, :, end_cols(q)])
+        y_buf[:, end_cols(q)] = y.astype(BF)
+        store_end(q).start()
+    for t in range(tiles - 1):
         store(t).wait()
+    for q in range(2):
+        store_end(q).wait()
 
 
 def params(limit=66_000_000):
@@ -401,8 +427,8 @@
             pltpu.VMEM((2, half // WIDE, WIDE, WIDE), BF),
             pltpu.VMEM((2, tokens, half), BF),
             pltpu.VMEM((tokens, cols), BF),
-            pltpu.SemaphoreType.DMA((2, tiles)),
-            pltpu.SemaphoreType.DMA((tiles,)),
+            pltpu.SemaphoreType.DMA((2, tiles + 1)),
+            pltpu.SemaphoreType.DMA((tiles + 1,)),
         ],
         compiler_params=params(limit=32 << 20),
         name="finish",

time: 52 us -> 52.7 us (1.013)
  Pallas kernels: 22.6 us -> 23.2 us
    pallas_call x1, Pallas kernels: 8.54 us -> 9.18 us  [call_finish(): pl.pallas_call(finish_kernel, in_specs=[pl.BlockSpec(memory_space=pltpu.S...]
where the time goes in v7:
time: 52.7 us; the launch traced here: 52.4 us
  Pallas kernels  23.2 us (44%)
  starting transfers between devices  17.3 us (33%)
  waiting for transfers between devices  11.9 us (23%)
    all_to_all x1, starting transfers between devices, shards(): msg = lax.all_to_all(msg, SEQ_HEAD, split_axis=0, concat_axis=0, tiled=True)  10.2 us
    pallas_call x2, Pallas kernels, call_local(): pl.pallas_call(local_kernel, in_specs=[pl.BlockSpec(memory_space=pltpu.SM...  9.67 us
    pallas_call x1, Pallas kernels, call_finish(): pl.pallas_call(finish_kernel, in_specs=[pl.BlockSpec(memory_space=pltpu.S...  9.18 us
    all_to_all x1, waiting for transfers between devices, shards(): lax.all_to_all(entering, SEQ_HEAD, split_axis=0, concat_axis=0, tiled=True)  6.21 us
    all_to_all x1, waiting for transfers between devices, shards(): msg = lax.all_to_all(msg, SEQ_HEAD, split_axis=0, concat_axis=0, tiled=True)  5.66 us
    all_to_all x1, starting transfers between devices, shards(): lax.all_to_all(entering, SEQ_HEAD, split_axis=0, concat_axis=0, tiled=True)  4.4 us
    pallas_call x1, Pallas kernels, call_state(): pl.pallas_call(state_kernel, in_specs=[any_block] * 3, out_specs=any_bloc...  3.41 us
    ppermute x1, starting transfers between devices, shards(): other_weight = lax.ppermute(weight, 'head', swap)  1.38 us
  transfers between devices with their start and end apart: 5, of which 2 were waited for; matrix products, arithmetic and copies ran while one was open for 0% of the time, Pallas kernels for 27%

profile of v7, /device:TPU:1, one launch (start us, length us, event | category | flops | bytes accessed | tf_op | source)
XLA Modules:
  0.0 52.4 jit_solution(11741422358025603892)
XLA Ops:
  0.0 0.0 copy-start
  0.0 0.0 copy-start.1
  0.0 1.4 %collective-permute-start.2 = (bf16[1024,4096]{1,0:T(8,128)(2,1)}, bf16[1024,4096]{1,0:T(8,128)(2,1)}, u32[]{:S(2)}, u32[]{:S(2)}) collective-permute-start(bf16[1024,4096]{1,0:T(8,128)(2,1)} %w1_hbm.1), channel_id=1, source_target_pairs={{0,1},{1,0},{2,3},{3,2},{4,5},{5,4},{6,7},{7,6},{8,9},{9,8},{10,11... | collective-permute-start | bytes 25165832 | tf_op jit(solution)/shard_map/ppermute | solution.py:444
  1.4 3.4 %state.1 = bf16[128,5,2,128]{3,2,1,0:T(2,128)(2,1)} custom-call(bf16[256,2048]{1,0:T(8,128)(2,1)} %k_hbm.5, bf16[256,2048]{1,0:T(8,128)(2,1)} %v_hbm.5, bf16[256,2048]{1,0:T(8,128)(2,1)} %w_hbm.5), custom_call_target="tpu_custom_call" | custom-call | flops 4294967296 | bytes 4194304 | tf_op jit(solution)/shard_map/state/pallas_call | solution.py:364
  4.8 10.2 %all-to-all-start = ((bf16[128,5,2,128]{3,2,1,0:T(2,128)(2,1)}), bf16[128,5,2,128]{3,2,1,0:T(2,128)(2,1)S(1)}, u32[]{:S(2)}, u32[]{:S(2)}) async-start(bf16[128,5,2,128]{3,2,1,0:T(2,128)(2,1)} %state.1), calls=%async_computation | async-start | bytes 655360 | tf_op jit(solution)/shard_map/all_to_all | solution.py:446
  15.0 0.0 copy-done
  15.0 0.0 copy-done.1
  15.1 4.8 %local.2 = (bf16[256,1024]{1,0:T(8,128)(2,1)S(1)}, bf16[256,1024]{1,0:T(8,128)(2,1)S(1)}, bf16[256,1024]{1,0:T(8,128)(2,1)S(1)}) custom-call(s32[1]{0:T(128)} %bitcast.h_ref.c_ref, f32[16,64]{1,0:T(8,128)S(1)} %copy-done, f32[1,1024]{1,0:T(1,128)S(1)} %bitcast.4, bf16[256,2048]{1,0:T(8,128)(2,1)} %r_hbm.3, bf16[256,2048]{1,0:T(8,128)(2,1)} %k_hbm.5, ...), custom_call_target="tpu_custom_call" | custom-call | flops 8589934592 | bytes 4194304 | tf_op jit(solution)/shard_map/local/pallas_call | solution.py:387
  19.9 1.2 %collective-permute-start.1 = (f32[1,1024]{1,0:T(1,128)S(1)}, f32[1,1024]{1,0:T(1,128)S(1)}, u32[]{:S(2)}, u32[]{:S(2)}) collective-permute-start(f32[1,1024]{1,0:T(1,128)S(1)} %bitcast.5), channel_id=1, source_target_pairs={{0,1},{1,0},{2,3},{3,2},{4,5},{5,4},{6,7},{7,6},{8,9},{9,8},{10,11... | collective-permute-start | bytes 12296 | tf_op jit(solution)/shard_map/ppermute | solution.py:451
  21.1 0.1 collective-permute-start
  21.1 5.7 %all-to-all-done.msg_ref = bf16[128,5,2,128]{3,2,1,0:T(2,128)(2,1)S(1)} async-done(((bf16[128,5,2,128]{3,2,1,0:T(2,128)(2,1)}), bf16[128,5,2,128]{3,2,1,0:T(2,128)(2,1)S(1)}, u32[]{:S(2)}, u32[]{:S(2)}) %all-to-all-start) | async-done | bytes 327712 | tf_op jit(solution)/shard_map/all_to_all | solution.py:446
  26.8 1.0 %scan.1 = bf16[128,8,128]{2,1,0:T(8,128)(2,1)} custom-call(bf16[128,5,2,128]{3,2,1,0:T(2,128)(2,1)S(1)} %all-to-all-done.msg_ref, bf16[256,1024]{1,0:T(8,128)(2,1)S(1)} %get-tuple-element.13.after_ref.mine_rin), custom_call_target="tpu_custom_call" | custom-call | tf_op jit(solution)/shard_map/scan/pallas_call | solution.py:401
  27.8 4.4 %all-to-all-start.1 = ((bf16[128,8,128]{2,1,0:T(8,128)(2,1)}), bf16[128,8,128]{2,1,0:T(8,128)(2,1)S(1)}, u32[]{:S(2)}, u32[]{:S(2)}) async-start(bf16[128,8,128]{2,1,0:T(8,128)(2,1)} %scan.1), calls=%async_computation.1 | async-start | bytes 524288 | tf_op jit(solution)/shard_map/all_to_all | solution.py:449
  32.2 0.0 collective-permute-done.1.gain_ref
  32.2 0.0 collective-permute-done.u_ref
  32.2 4.8 %local.3 = (bf16[256,1024]{1,0:T(8,128)(2,1)S(1)}, bf16[256,1024]{1,0:T(8,128)(2,1)S(1)}, bf16[256,1024]{1,0:T(8,128)(2,1)S(1)}) custom-call(s32[1]{0:T(128)S(6)} %sub.3.h_ref, f32[16,64]{1,0:T(8,128)S(1)} %collective-permute-done.u_ref, f32[1,1024]{1,0:T(1,128)S(1)} %collective-permute-done.1.gain_ref, bf16[256,2048]{1,0:T(8,128)(2,1)} %r_hbm.3, ...), custom_call_target="tpu_custom_call" | custom-call | flops 8589934592 | bytes 4194304 | tf_op jit(solution)/shard_map/local/pallas_call | solution.py:387
  37.0 6.2 %all-to-all-done.1 = bf16[128,8,128]{2,1,0:T(8,128)(2,1)S(1)} async-done(((bf16[128,8,128]{2,1,0:T(8,128)(2,1)}), bf16[128,8,128]{2,1,0:T(8,128)(2,1)S(1)}, u32[]{:S(2)}, u32[]{:S(2)}) %all-to-all-start.1) | async-done | bytes 262176 | tf_op jit(solution)/shard_map/all_to_all | solution.py:449
  43.3 0.0 collective-permute-done.2.w2_hbm
  43.3 9.2 %finish.1 = bf16[256,4096]{1,0:T(8,128)(2,1)} custom-call(s32[1]{0:T(128)} %bitcast.h_ref.c_ref, bf16[16,64,128]{2,1,0:T(8,128)(2,1)S(1)} %bitcast.3, bf16[256,1024]{1,0:T(8,128)(2,1)S(1)} %get-tuple-element.14.mine_out, bf16[256,1024]{1,0:T(8,128)(2,1)S(1)} %get-tuple-element.13.after_ref.mine_rin, bf16[256,1024]{1,0:T(8,128)(2,1)S(1)} %get-tuple-element.15.mine_sg, ...), custom_call_target="tpu_custom_call" | custom-call | tf_op jit(solution)/shard_map/finish/pallas_call | solution.py:417
Async XLA Ops:
  0.0 15.0 %copy-start = (f32[16,64]{1,0:T(8,128)S(1)}, f32[16,64]{1,0:T(8,128)}, u32[]{:S(2)}) copy-start(f32[16,64]{1,0:T(8,128)} %u_ref.1) | copy-start | bytes 12292
  0.0 15.0 %copy-start.1 = (f32[1024]{0:T(1024)S(1)}, f32[1024]{0:T(1024)}, u32[]{:S(2)}) copy-start(f32[1024]{0:T(1024)} %param.14) | copy-start | bytes 12292
  0.0 43.3 %collective-permute-start.2 = (bf16[1024,4096]{1,0:T(8,128)(2,1)}, bf16[1024,4096]{1,0:T(8,128)(2,1)}, u32[]{:S(2)}, u32[]{:S(2)}) collective-permute-start(bf16[1024,4096]{1,0:T(8,128)(2,1)} %w1_hbm.1), channel_id=1, source_target_pairs={{0,1},{1,0},{2,3},{3,2},{4,5},{5,4},{6,7},{7,6},{8,9},{9,8},{10,11... | collective-permute-start | bytes 25165832 | tf_op jit(solution)/shard_map/ppermute | solution.py:444
  4.8 22.0 %all-to-all-start = ((bf16[128,5,2,128]{3,2,1,0:T(2,128)(2,1)}), bf16[128,5,2,128]{3,2,1,0:T(2,128)(2,1)S(1)}, u32[]{:S(2)}, u32[]{:S(2)}) async-start(bf16[128,5,2,128]{3,2,1,0:T(2,128)(2,1)} %state.1), calls=%async_computation | async-start | bytes 655360 | tf_op jit(solution)/shard_map/all_to_all | solution.py:446
  19.9 12.3 %collective-permute-start.1 = (f32[1,1024]{1,0:T(1,128)S(1)}, f32[1,1024]{1,0:T(1,128)S(1)}, u32[]{:S(2)}, u32[]{:S(2)}) collective-permute-start(f32[1,1024]{1,0:T(1,128)S(1)} %bitcast.5), channel_id=1, source_target_pairs={{0,1},{1,0},{2,3},{3,2},{4,5},{5,4},{6,7},{7,6},{8,9},{9,8},{10,11... | collective-permute-start | bytes 12296 | tf_op jit(solution)/shard_map/ppermute | solution.py:451
  21.1 11.1 %collective-permute-start = (f32[16,64]{1,0:T(8,128)S(1)}, f32[16,64]{1,0:T(8,128)S(1)}, u32[]{:S(2)}, u32[]{:S(2)}) collective-permute-start(f32[16,64]{1,0:T(8,128)S(1)} %copy-done), channel_id=1, source_target_pairs={{0,1},{1,0},{2,3},{3,2},{4,5},{5,4},{6,7},{7,6},{8,9},{9,8},{10,11... | collective-permute-start | bytes 12296 | tf_op jit(solution)/shard_map/ppermute | solution.py:451
  27.8 15.5 %all-to-all-start.1 = ((bf16[128,8,128]{2,1,0:T(8,128)(2,1)}), bf16[128,8,128]{2,1,0:T(8,128)(2,1)S(1)}, u32[]{:S(2)}, u32[]{:S(2)}) async-start(bf16[128,8,128]{2,1,0:T(8,128)(2,1)} %scan.1), calls=%async_computation.1 | async-start | bytes 524288 | tf_op jit(solution)/shard_map/all_to_all | solution.py:449
